TPU v7x, 32 devices: a whole 2x2x4 slice. The times are simulated.
32 devices in a mesh: sample: 2 (over x), fsdp: 4 (over z), seq: 4 (over y, core).
Axes of the slice: x: 2, y: 2, z: 4, core: 2. Of those that a mesh axis runs over, the one named last changes fastest.
Arguments:
- token_act: bfloat16 [8, 512, 768], P(('sample', 'fsdp'), 'seq'), may hold values from -40 to 40
- token_cond: bfloat16 [8, 512, 768], P(('sample', 'fsdp'), 'seq'), may hold values from -40 to 40
- pair_bias: bfloat16 [16, 512, 512], P('fsdp', 'seq'), may hold values from -8 to 296
- token_mask: int32 [512], P('seq'), may hold values 0 or 1
- ada_weights: bfloat16 [4, 768, 768], P(None, None, 'fsdp'), may hold values from -0.21875 to 0.21875
- attention_in: bfloat16 [4, 768, 768], P(None, None, 'fsdp'), may hold values from -0.21875 to 0.21875
- attention_out: bfloat16 [768, 768], P('fsdp'), may hold values from -0.21875 to 0.21875
- transition_in: bfloat16 [2, 768, 1536], P(None, None, 'fsdp'), may hold values from -0.21875 to 0.21875
- transition_out: bfloat16 [1536, 768], P('fsdp'), may hold values from -0.15625 to 0.15625
- token_vectors: float32 [3, 768], replicated, may hold values from -4 to 4
- atom_skip: bfloat16 [8, 4096, 128], P(('sample', 'fsdp'), 'seq'), may hold values from -40 to 40
- atom_cond: bfloat16 [4096, 128], P('seq'), may hold values from -40 to 40
- atom_bias: bfloat16 [4, 4096, 128], P(None, 'seq'), may hold values from -6 to 296
- window_bounds: int32 [128, 2], P('seq'), may hold values from 0 to 4096, as said below
- atom_token: int32 [4096], P('seq'), may hold values from 0 to 511, as said below
- atom_weights: bfloat16 [7, 128, 128], P(None, None, 'fsdp'), may hold values from -0.5 to 0.5
- token_to_atom: bfloat16 [768, 128], P('fsdp'), may hold values from -0.21875 to 0.21875
- atom_vectors: float32 [2, 128], replicated, may hold values from -4 to 4
- position_out: bfloat16 [3, 128], replicated, may hold values from -0.5 to 0.5
Outputs:
- token_out: bfloat16 [8, 512, 768], P(('sample', 'fsdp'), 'seq')
- position_update: float32 [8, 3, 4096], P(('sample', 'fsdp'), None, 'seq')
Inputs may be any that keep to these rules, and one draw needn't show every extreme that they name: `window_bounds`: row b belongs to the atoms 32 * b to 32 * b + 31; column 0 is at least 0 and at least 32 * b - 48, and at most 32 * b; column 1 is at least 32 * b + 32, at most 32 * b + 80 and at most 4096. `atom_token`: atoms are numbered in token order: the value never falls from one atom to the next, the first atom belongs to token 0, the last to token 511, and every token owns 1 to 24 atoms.
All inputs are finite; a program needn't handle non-finite values. No bound on the sum of `token_mask` on one device may be relied on, other than what follows from the above.
Results may differ from a plain program's by a relative error of at most 0.014.
Values may be sent and summed in bfloat16 or wider, within the bound.
A program may use at most 128 MiB of HBM per device.

v0:
```python
import math

import jax
import jax.numpy as jnp
from jax import lax
from jax.sharding import PartitionSpec as P

HA = 4
WQ = 32
WK = 128
HD = 48


EPS = 1e-05
FAR = -1e30


def extended(array, sides, width):
    for axis, dim in sides:
        size, length = (lax.axis_size(axis), array.shape[dim])
        up = [(i, (i + 1) % size) for i in range(size - 1)]
        down = [(j, i) for i, j in up]
        last = lax.slice_in_dim(array, length - width, length, axis=dim)
        first = lax.slice_in_dim(array, 0, width, axis=dim)
        before = lax.ppermute(last, axis, up)
        after = lax.ppermute(first, axis, down)
        array = jnp.concatenate([before, array, after], axis=dim)
    return array


def layer_norm(values):
    values = values.astype(jnp.float32)
    center = values - jnp.mean(values, axis=-1, keepdims=True)
    spread = jnp.mean(center * center, axis=-1, keepdims=True)
    return center * lax.rsqrt(spread + EPS)


def matmul(left_side, right_side):
    return jnp.dot(left_side, right_side, preferred_element_type=jnp.float32)


def adaptive(values, normed_cond, scale_weight, shift_weight, offset):
    return jax.nn.sigmoid(matmul(normed_cond, scale_weight) + offset) * layer_norm(values) + matmul(
        normed_cond, shift_weight
    )


def absorb(running, queries, key_rows, value_rows, live_keys, bias_block, score_scale):
    maxima, totals, summed = running
    scores = (
        jnp.einsum("tshd,ushd->shtu", queries, key_rows, preferred_element_type=jnp.float32)
        * score_scale
    )
    scores = scores + bias_block[None].astype(jnp.float32)
    scores = jnp.where(live_keys[None, None, None, :] > 0, scores, FAR)
    new_maxima = jnp.maximum(maxima, jnp.max(scores, axis=-1))
    factor = jnp.exp(maxima - new_maxima)
    weights = jnp.exp(scores - new_maxima[..., None])
    totals = totals * factor + jnp.sum(weights, axis=-1)
    update = jnp.einsum(
        "shtu,ushd->tshd",
        weights.astype(jnp.bfloat16),
        value_rows,
        preferred_element_type=jnp.float32,
    )
    summed = summed * jnp.transpose(factor, (2, 0, 1))[..., None] + update
    return (new_maxima, totals, summed)


def token_attention(query_rows, key_rows, value_rows, gate_rows, pair_bias, token_mask, groups):
    row_count = query_rows.shape[0]
    heads_here = pair_bias.shape[0]
    queries = query_rows.reshape(row_count, groups, heads_here, HD)
    score_scale = 1.0 / math.sqrt(HD)
    key_block = 512

    def absorb_piece(running, piece_data):
        piece_keys, piece_values, piece_live = piece_data
        piece_rows = piece_keys.shape[0]
        piece_keys = piece_keys.reshape(piece_rows, groups, heads_here, HD)
        piece_values = piece_values.reshape(piece_rows, groups, heads_here, HD)
        if piece_rows > key_block and piece_rows % key_block == 0:

            def absorb_block(state_now, step_index):
                offset = step_index * key_block
                return (
                    absorb(
                        state_now,
                        queries,
                        lax.dynamic_slice_in_dim(piece_keys, offset, key_block, 0),
                        lax.dynamic_slice_in_dim(piece_values, offset, key_block, 0),
                        lax.dynamic_slice_in_dim(piece_live, offset, key_block, 0),
                        lax.dynamic_slice_in_dim(pair_bias, offset, key_block, 2),
                        score_scale,
                    ),
                    None,
                )

            running, unused = lax.scan(
                absorb_block, running, jnp.arange(piece_rows // key_block, dtype=jnp.int32)
            )
            return running
        return absorb(
            running, queries, piece_keys, piece_values, piece_live, pair_bias, score_scale
        )

    initial = (
        jnp.full((groups, heads_here, row_count), FAR, jnp.float32),
        jnp.zeros((groups, heads_here, row_count), jnp.float32),
        jnp.zeros((row_count, groups, heads_here, HD), jnp.float32),
    )
    maxima, totals, summed = absorb_piece(
        initial,
        (
            lax.all_gather(key_rows, "seq", axis=0, tiled=True),
            lax.all_gather(value_rows, "seq", axis=0, tiled=True),
            lax.all_gather(token_mask, "seq", axis=0, tiled=True),
        ),
    )
    attended = summed / jnp.transpose(totals, (2, 0, 1))[..., None]
    attended = attended.reshape(row_count, groups * heads_here * HD)
    return (attended * jax.nn.sigmoid(gate_rows.astype(jnp.float32))).astype(jnp.bfloat16)


def window_attention(queries, padded, bias_rows, bounds, first_atom):
    atom_count, feature_count = queries.shape
    block_count = atom_count // WQ
    step_count = WK // WQ
    rim_width = (WK - WQ) // 2
    head_width = feature_count // HA
    tile_rows = padded.reshape(block_count + step_count - 1, WQ, 2 * feature_count)
    windows = jnp.concatenate(
        [tile_rows[position : position + block_count] for position in range(step_count)], axis=1
    )
    key_rows = windows[:, :, :feature_count].reshape(block_count, WK, HA, head_width)
    value_rows = windows[:, :, feature_count:].reshape(block_count, WK, HA, head_width)
    query_rows = queries.reshape(block_count, WQ, HA, head_width)
    scores = jnp.einsum(
        "bqhd,bkhd->hbqk", query_rows, key_rows, preferred_element_type=jnp.float32
    ) * (1.0 / math.sqrt(head_width))
    scores = scores + bias_rows.reshape(HA, block_count, WQ, WK).astype(jnp.float32)
    slot_atoms = (
        first_atom
        + WQ * jnp.arange(block_count, dtype=jnp.int32)[:, None]
        - rim_width
        + jnp.arange(WK, dtype=jnp.int32)[None, :]
    )
    in_window = (slot_atoms >= bounds[:, 0:1]) & (slot_atoms < bounds[:, 1:2])
    scores = jnp.where(in_window[None, :, None, :], scores, FAR)
    maxima = jnp.max(scores, axis=-1, keepdims=True)
    weights = jnp.exp(scores - maxima)
    totals = jnp.sum(weights, axis=-1)
    attended = jnp.einsum(
        "hbqk,bkhd->bqhd",
        weights.astype(jnp.bfloat16),
        value_rows,
        preferred_element_type=jnp.float32,
    )
    attended = attended / jnp.transpose(totals, (1, 2, 0))[..., None]
    return attended.reshape(atom_count, feature_count)


def per_device(
    token_act,
    token_cond,
    pair_bias,
    token_mask,
    ada_weights,
    attention_in,
    attention_out,
    transition_in,
    transition_out,
    token_vectors,
    atom_skip,
    atom_cond,
    atom_bias,
    window_bounds,
    atom_token,
    atom_weights,
    token_to_atom,
    atom_vectors,
    position_out,
):
    groups = lax.axis_size("fsdp")
    act_rows = token_act[0]
    row_count = act_rows.shape[0]
    cond_normed = layer_norm(token_cond[0]).astype(jnp.bfloat16)
    ada_full, atom_full, project_full = (
        lax.all_gather(ada_weights, "fsdp", axis=2, tiled=True),
        lax.all_gather(atom_weights, "fsdp", axis=2, tiled=True),
        lax.all_gather(token_to_atom, "fsdp", axis=0, tiled=True),
    )
    attend_x = adaptive(act_rows, cond_normed, ada_full[0], ada_full[1], token_vectors[0]).astype(
        jnp.bfloat16
    )
    transit_x = adaptive(act_rows, cond_normed, ada_full[2], ada_full[3], token_vectors[1]).astype(
        jnp.bfloat16
    )
    gathered = (
        lax.all_gather(attend_x, "fsdp", axis=1, tiled=True),
        lax.all_gather(transit_x, "fsdp", axis=1, tiled=True),
    )
    attend_all = gathered[0].reshape(row_count, groups, -1)
    transit_all = gathered[1].reshape(row_count, groups, -1)
    column_count = attention_in.shape[2]
    query_bias = lax.dynamic_slice_in_dim(
        token_vectors[2], lax.axis_index("fsdp") * column_count, column_count
    )

    def project(weight_cols):
        return jnp.einsum(
            "tsd,dc->tsc", attend_all, weight_cols, preferred_element_type=jnp.float32
        )

    query_rows = (project(attention_in[0]) + query_bias).astype(jnp.bfloat16).reshape(row_count, -1)
    key_rows = project(attention_in[1]).astype(jnp.bfloat16).reshape(row_count, -1)
    value_rows = project(attention_in[2]).astype(jnp.bfloat16).reshape(row_count, -1)
    gate_rows = project(attention_in[3]).astype(jnp.bfloat16).reshape(row_count, -1)
    gate_part = jnp.einsum(
        "tsd,df->tsf", transit_all, transition_in[0], preferred_element_type=jnp.float32
    )
    up_part = jnp.einsum(
        "tsd,df->tsf", transit_all, transition_in[1], preferred_element_type=jnp.float32
    )
    hidden = (jax.nn.silu(gate_part) * up_part).astype(jnp.bfloat16)
    gated = token_attention(
        query_rows, key_rows, value_rows, gate_rows, pair_bias, token_mask, groups
    )
    partial_sum = jnp.einsum(
        "tsc,cd->tsd",
        gated.reshape(row_count, groups, column_count),
        attention_out,
        preferred_element_type=jnp.float32,
    )
    partial_sum = partial_sum + jnp.einsum(
        "tsf,fd->tsd", hidden, transition_out, preferred_element_type=jnp.float32
    )
    combined = (
        lax.psum_scatter(partial_sum.astype(jnp.bfloat16), "fsdp", scatter_dimension=1, tiled=True)
        .astype(jnp.float32)
        .reshape(row_count, -1)
    )
    token_result = (act_rows.astype(jnp.float32) + combined).astype(jnp.bfloat16)
    projected = matmul(token_result, project_full).astype(jnp.bfloat16)
    all_rows = lax.all_gather(projected, "seq", axis=0, tiled=True)
    atom_state = atom_skip[0].astype(jnp.float32) + jnp.take(all_rows, atom_token, axis=0).astype(
        jnp.float32
    )
    atom_normed = layer_norm(atom_cond).astype(jnp.bfloat16)
    atom_x = adaptive(atom_state, atom_normed, atom_full[0], atom_full[1], atom_vectors[0]).astype(
        jnp.bfloat16
    )
    atom_query = (matmul(atom_x, atom_full[2]) + atom_vectors[1]).astype(jnp.bfloat16)
    atom_key = matmul(atom_x, atom_full[3]).astype(jnp.bfloat16)
    atom_value = matmul(atom_x, atom_full[4]).astype(jnp.bfloat16)
    atom_gate = matmul(atom_x, atom_full[5]).astype(jnp.bfloat16)
    pairs = jnp.concatenate([atom_key, atom_value], axis=1)
    rim_width = (WK - WQ) // 2
    padded = extended(pairs, (("seq", 0),), rim_width)
    atom_count = atom_query.shape[0]
    first_atom = lax.axis_index("seq") * atom_count
    atom_attended = window_attention(atom_query, padded, atom_bias, window_bounds, first_atom)
    atom_gated = (atom_attended * jax.nn.sigmoid(atom_gate.astype(jnp.float32))).astype(
        jnp.bfloat16
    )
    atom_new = atom_state + matmul(atom_gated, atom_full[6])
    final_normed = layer_norm(atom_new).astype(jnp.bfloat16)
    update = lax.dot_general(
        position_out, final_normed, (((1,), (1,)), ((), ())), preferred_element_type=jnp.float32
    )
    return (token_result[None], update[None])


def solution(mesh):
    in_specs = (
        P(("sample", "fsdp"), "seq", None),
        P(("sample", "fsdp"), "seq", None),
        P("fsdp", "seq", None),
        P("seq"),
        P(None, None, "fsdp"),
        P(None, None, "fsdp"),
        P("fsdp", None),
        P(None, None, "fsdp"),
        P("fsdp", None),
        P(),
        P(("sample", "fsdp"), "seq", None),
        P("seq", None),
        P(None, "seq", None),
        P("seq", None),
        P("seq"),
        P(None, None, "fsdp"),
        P("fsdp", None),
        P(),
        P(),
    )
    out_specs = (P(("sample", "fsdp"), "seq", None), P(("sample", "fsdp"), None, "seq"))
    return jax.shard_map(
        per_device, mesh=mesh, in_specs=in_specs, out_specs=out_specs, check_vma=False
    )
```

profile of v0, /device:TPU:1, one launch (start us, length us, event | category | flops | bytes accessed | tf_op | source)
XLA Modules:
  0.0 255.2 jit_solution(12503067049552430213)
XLA Ops:
  9.2 5.9 %all-gather = s32[4,1,128]{2,1,0:T(1,128)S(1)} all-gather(s32[1,1,128]{2,1,0:T(1,128)S(1)} %bitcast.220), channel_id=1, replica_groups=mesh['sample'=2,'fsdp'=4,'seq'=4] {'seq'}, dimensions={0}, use_global_device_ids=true | all-gather | bytes 2560 | tf_op jit(solution)/shard_map/all_gather | solution.py:117
  16.1 85.0 %all-gather.3.cloned.1.call-done = bf16[4,768,768]{1,2,0:T(8,128)(2,1)} async-done(((bf16[4,768,192]{1,2,0:T(8,128)(2,1)}), bf16[4,768,768]{1,2,0:T(8,128)(2,1)}) %all-gather.3.cloned.1.call-update) | async-done | bytes 4718608 | tf_op jit(solution)/shard_map/all_gather | solution.py:189
  101.0 1.8 fusion.32
  102.9 1.9 fusion.40
  104.8 16.1 %all_gather.29 = bf16[128,3072]{1,0:T(8,128)(2,1)S(1)} all-gather(bf16[128,768]{1,0:T(8,128)(2,1)S(1)} %fusion.40), channel_id=1, replica_groups=mesh['sample'=2,'fsdp'=4,'seq'=4] {'fsdp'}, dimensions={1}, use_global_device_ids=true | all-gather | bytes 983040 | tf_op jit(solution)/shard_map/all_gather | solution.py:200
  122.2 11.0 %all_gather.30 = bf16[512,768]{0,1:T(8,128)(2,1)S(1)} all-gather(bf16[128,768]{0,1:T(8,128)(2,1)S(1)} %bitcast.214), channel_id=1, replica_groups=mesh['sample'=2,'fsdp'=4,'seq'=4] {'seq'}, dimensions={0}, use_global_device_ids=true | all-gather | bytes 983040 | tf_op jit(solution)/shard_map/all_gather | solution.py:115
  133.1 8.7 %all_gather.31 = bf16[512,768]{0,1:T(8,128)(2,1)S(1)} all-gather(bf16[128,768]{0,1:T(8,128)(2,1)S(1)} %bitcast.213), channel_id=1, replica_groups=mesh['sample'=2,'fsdp'=4,'seq'=4] {'seq'}, dimensions={0}, use_global_device_ids=true | all-gather | bytes 983040 | tf_op jit(solution)/shard_map/all_gather | solution.py:116
  143.0 16.2 %all_gather.32 = bf16[128,3072]{1,0:T(8,128)(2,1)S(1)} all-gather(bf16[128,768]{1,0:T(8,128)(2,1)S(1)} %fusion.41), channel_id=1, replica_groups=mesh['sample'=2,'fsdp'=4,'seq'=4] {'fsdp'}, dimensions={1}, use_global_device_ids=true | all-gather | bytes 983040 | tf_op jit(solution)/shard_map/all_gather | solution.py:201
  161.7 1.5 fusion.58
  163.1 2.1 fusion.53
  165.2 3.2 %fusion.49 = f32[128,4,768]{2,0,1:T(8,128)} fusion(f32[128,4,192]{0,2,1:T(8,128)} %bitcast.222, bf16[16,4,8,768]{3,2,1,0:T(8,128)(2,1)S(1)} %bitcast.208, bf16[192,768]{1,0:T(8,128)(2,1)S(1)} %copy-done.21, bf16[4,768,192]{1,2,0:T(8,128)(2,1)} %param.24), kind=kOutput, calls=%fused_computation.72 | convolution fusion | flops 302678016 | bytes 3342336 | tf_op jit(solution)/shard_map/tsc,cd->tsd/dot_general | solution.py:229
  168.5 3.9 %add_convert_fusion = bf16[128,4,768]{2,0,1:T(8,128)(2,1)} fusion(f32[128,4,768]{2,0,1:T(8,128)} %fusion.49, f32[128,4,384]{2,0,1:T(8,128)} %fusion.58, bf16[16,4,8,768]{3,2,1,0:T(8,128)(2,1)S(1)} %bitcast.211, bf16[384,768]{1,0:T(8,128)(2,1)S(1)} %copy-done, bf16[2,768,384]{2,1,0:T(8,128)(2,1)} %param.26), kind=kOutput, calls=%fused_computation.14 | convolution fusion | flops 605945856 | bytes 5111808 | tf_op jit(solution)/shard_map/tsf,fd->tsd/dot_general | solution.py:235
  172.4 12.7 %all_gather.33 = bf16[768,128]{1,0:T(8,128)(2,1)S(1)} all-gather(bf16[192,128]{1,0:T(8,128)(2,1)S(1)} %copy-done.11), channel_id=1, replica_groups=mesh['sample'=2,'fsdp'=4,'seq'=4] {'fsdp'}, dimensions={0}, use_global_device_ids=true | all-gather | bytes 245760 | tf_op jit(solution)/shard_map/all_gather | solution.py:191
  185.1 14.0 %all_gather.35 = bf16[7,128,128]{1,2,0:T(8,128)(2,1)S(1)} all-gather(bf16[7,128,32]{1,2,0:T(8,128)(2,1)S(1)} %copy-done.10), channel_id=1, replica_groups=mesh['sample'=2,'fsdp'=4,'seq'=4] {'fsdp'}, dimensions={2}, use_global_device_ids=true | all-gather | bytes 286720 | tf_op jit(solution)/shard_map/all_gather | solution.py:190
  200.8 11.9 %all_gather.34 = bf16[512,128]{1,0:T(8,128)(2,1)S(1)} all-gather(bf16[128,128]{1,0:T(8,128)(2,1)S(1)} %convolution_convert_fusion.6), channel_id=1, replica_groups=mesh['sample'=2,'fsdp'=4,'seq'=4] {'seq'}, dimensions={0}, use_global_device_ids=true | all-gather | bytes 163840 | tf_op jit(solution)/shard_map/all_gather | solution.py:245
  212.7 3.2 %gather_fusion = bf16[1024,128]{1,0:T(8,128)(2,1)S(1)} fusion(bf16[512,128]{1,0:T(8,128)(2,1)S(1)} %all_gather.34, s32[1024]{0:T(1024)S(1)} %fusion.123), kind=kCustom, calls=%fused_computation | custom fusion | bytes 528384 | tf_op jit(solution)/shard_map/jit(_take)/gather | solution.py:246
  218.6 2.2 collective-permute-start
  220.8 2.1 collective-permute-start.1
  223.9 1.4 reshape.261
  234.0 3.7 %fusion.135 = (f32[4,32,32]{2,1,0:T(8,128)S(1)}, bf16[4,32,32,128]{3,2,1,0:T(8,128)(2,1)}) fusion(bf16[4,32,32,128]{3,2,1,0:T(8,128)(2,1)} %bitcast.221, bf16[32,128,4,32]{1,3,2,0:T(8,128)(2,1)} %bitcast.203, bf16[32,32,4,32]{3,2,1,0:T(4,128)(2,1)} %reshape.261, pred[32,128]{1,0:T(8,128)(4,1)S(1)} %fusion.122), kind=kOutput, calls=%fused_computation.194 | convolution fusion | flops 37224576 | bytes 3428352 | tf_op jit(solution)/shard_map/sub | solution.py:151
  238.4 3.2 %bitcast_divide_fusion = f32[32,32,4,32]{1,3,2,0:T(8,128)} fusion(bf16[32,128,4,32]{1,3,2,0:T(8,128)(2,1)S(1)} %bitcast.204, bf16[4,32,32,128]{3,2,1,0:T(8,128)(2,1)} %get-tuple-element.11, f32[32,32,4]{1,2,0:T(4,128)S(1)} %copy.62), kind=kOutput, calls=%fused_computation.10 | convolution fusion | flops 33685504 | bytes 2637824 | tf_op jit(solution)/shard_map/hbqk,bkhd->bqhd/dot_general | solution.py:153
  241.6 2.1 copy.63
  243.7 1.7 reshape.263
  245.3 1.6 fusion.139
  (110 shorter events, 23.7 us)
Async XLA Ops:
  7.2 161.3 %copy-start = (bf16[384,768]{1,0:T(8,128)(2,1)S(1)}, bf16[384,768]{1,0:T(8,128)(2,1)}, u32[]{:S(2)}) copy-start(bf16[384,768]{1,0:T(8,128)(2,1)} %param.27) | copy-start | bytes 1769476
  7.2 2.0 copy-start.17
  7.2 7.9 %copy-start.13 = (f32[3,768]{1,0:T(4,128)S(1)}, f32[3,768]{1,0:T(4,128)}, u32[]{:S(2)}) copy-start(f32[3,768]{1,0:T(4,128)} %param.28) | copy-start | bytes 27652
  7.2 8.0 %copy-start.1 = (bf16[1,128,768]{2,1,0:T(8,128)(2,1)S(1)}, bf16[1,128,768]{2,1,0:T(8,128)(2,1)}, u32[]{:S(2)}) copy-start(bf16[1,128,768]{2,1,0:T(8,128)(2,1)} %param.19) | copy-start | bytes 589828
  7.2 8.1 %copy-start.5 = (bf16[1,128,768]{2,1,0:T(8,128)(2,1)S(1)}, bf16[1,128,768]{2,1,0:T(8,128)(2,1)}, u32[]{:S(2)}) copy-start(bf16[1,128,768]{2,1,0:T(8,128)(2,1)} %param.20) | copy-start | bytes 589828
  7.2 8.2 %copy-start.2 = (bf16[1024,128]{1,0:T(8,128)(2,1)S(1)}, bf16[1024,128]{1,0:T(8,128)(2,1)}, u32[]{:S(2)}) copy-start(bf16[1024,128]{1,0:T(8,128)(2,1)} %param.30) | copy-start | bytes 786436
  7.2 93.8 %all-gather.3.cloned.1.call-start = ((), (), s32[]{:S(2)}) async-start(), calls=%async_computation.1 | async-start | bytes 5898240 | tf_op jit(solution)/shard_map/all_gather | solution.py:189
  8.0 191.7 %reduce-scatter.2.cloned.1.call-start = ((), (), s32[]{:S(2)}) async-start(), calls=%async_computation.2 | async-start | bytes 983040 | tf_op jit(solution)/shard_map/reduce_scatter | solution.py:239
  102.9 18.0 %copy-start.19 = (bf16[4,768,192]{1,2,0:T(8,128)(2,1)S(1)}, bf16[4,768,192]{1,2,0:T(8,128)(2,1)}, u32[]{:S(2)}) copy-start(bf16[4,768,192]{1,2,0:T(8,128)(2,1)} %param.24) | copy-start | bytes 3538948
  121.3 20.5 %copy-start.18 = (bf16[4,768,768]{1,2,0:T(8,128)(2,1)S(1)}, bf16[4,768,768]{1,2,0:T(8,128)(2,1)}, u32[]{:S(2)}) copy-start(bf16[4,768,768]{1,2,0:T(8,128)(2,1)} %all-gather.3.cloned.1.call-done) | copy-start | bytes 14155780
  159.2 2.5 copy-start.7
  163.1 2.1 copy-start.21
  165.2 3.2 %copy-start.8 = (bf16[128,3072]{1,0:T(8,128)(2,1)S(1)}, bf16[128,3072]{1,0:T(8,128)(2,1)}, u32[]{:S(2)}) copy-start(bf16[128,3072]{1,0:T(8,128)(2,1)} %copy-done.7) | copy-start | bytes 2359300
  168.5 3.9 %copy-start.11 = (bf16[192,128]{1,0:T(8,128)(2,1)S(1)}, bf16[192,128]{1,0:T(8,128)(2,1)}, u32[]{:S(2)}) copy-start(bf16[192,128]{1,0:T(8,128)(2,1)} %param.35) | copy-start | bytes 147460
  168.5 16.6 %copy-start.10 = (bf16[7,128,32]{1,2,0:T(8,128)(2,1)S(1)}, bf16[7,128,32]{1,2,0:T(8,128)(2,1)}, u32[]{:S(2)}) copy-start(bf16[7,128,32]{1,2,0:T(8,128)(2,1)} %param.34) | copy-start | bytes 172036
  168.5 31.0 %copy-start.15 = (s32[32,2]{0,1:T(2,128)S(1)}, s32[32,2]{0,1:T(2,128)}, u32[]{:S(2)}) copy-start(s32[32,2]{0,1:T(2,128)} %param.32) | copy-start | bytes 772
  168.5 31.0 %copy-start.16 = (f32[2,128]{1,0:T(2,128)S(1)}, f32[2,128]{1,0:T(2,128)}, u32[]{:S(2)}) copy-start(f32[2,128]{1,0:T(2,128)} %param.36) | copy-start | bytes 3076
  168.5 31.0 %copy-start.12 = (s32[1024]{0:T(1024)S(1)}, s32[1024]{0:T(1024)}, u32[]{:S(2)}) copy-start(s32[1024]{0:T(1024)} %param.33) | copy-start | bytes 12292
  172.4 43.5 %copy-start.4 = (bf16[1,1024,128]{2,1,0:T(8,128)(2,1)S(1)}, bf16[1,1024,128]{2,1,0:T(8,128)(2,1)}, u32[]{:S(2)}) copy-start(bf16[1,1024,128]{2,1,0:T(8,128)(2,1)} %param.29) | copy-start | bytes 786436
  199.1 24.5 %copy-start.9 = (bf16[7,128,128]{1,2,0:T(8,128)(2,1)}, bf16[7,128,128]{1,2,0:T(8,128)(2,1)S(1)}, u32[]{:S(2)}) copy-start(bf16[7,128,128]{1,2,0:T(8,128)(2,1)S(1)} %all_gather.35) | copy-start | bytes 688132
  217.5 5.4 %copy-start.6 = (bf16[128,1,768]{2,0,1:T(8,128)(2,1)S(1)}, bf16[128,1,768]{2,0,1:T(8,128)(2,1)}, u32[]{:S(2)}) copy-start(bf16[128,1,768]{2,0,1:T(8,128)(2,1)} %reduce-scatter.2.cloned.1.call-done) | copy-start | bytes 589828
  218.6 6.7 %collective-permute-start = (bf16[48,256]{0,1:T(8,128)(2,1)S(1)}, bf16[48,256]{0,1:T(8,128)(2,1)S(1)}, u32[]{:S(2)}, u32[]{:S(2)}) collective-permute-start(bf16[48,256]{0,1:T(8,128)(2,1)S(1)} %get-tuple-element.20), channel_id=1, source_target_pairs={{0,1},{1,2},{2,3},{4,5},{5,6},{6,7},{8,9},{9,10},{10,11},{12,13},{... | collective-permute-start | bytes 73736 | tf_op jit(solution)/shard_map/ppermute | solution.py:25
  220.8 5.6 %collective-permute-start.1 = (bf16[48,256]{0,1:T(8,128)(2,1)S(1)}, bf16[48,256]{0,1:T(8,128)(2,1)S(1)}, u32[]{:S(2)}, u32[]{:S(2)}) collective-permute-start(bf16[48,256]{0,1:T(8,128)(2,1)S(1)} %get-tuple-element.21), channel_id=1, source_target_pairs={{1,0},{2,1},{3,2},{5,4},{6,5},{7,6},{9,8},{10,9},{11,10},{13,12},{... | collective-permute-start | bytes 73736 | tf_op jit(solution)/shard_map/ppermute | solution.py:26
  245.3 2.0 copy-start.14
  (2 other events, 2.6 us)
Sparse Core Ops, SparseCore 0:
  9.6 91.3 all-gather.2
  172.5 26.3 reduce-scatter.1
where the time goes:
time: 256 us; the launch traced here: 255 us
  blocking collectives  96.4 us (38%)
  waiting for transfers between devices  86.8 us (34%)
  matrix products  29.8 us (12%)
  local copies, waits for them, and re-layouts  15.7 us (6%)
  between operations  14.6 us (6%)
  other arithmetic  7.49 us (3%)
  starting transfers between devices  4.4 us (2%)
    all_gather x1, waiting for transfers between devices, per_device(): lax.all_gather(ada_weights, 'fsdp', axis=2, tiled=True)  85 us
    all_gather x1, blocking collectives, per_device(): lax.all_gather(transit_x, 'fsdp', axis=1, tiled=True)  16.2 us
    all_gather x1, blocking collectives, per_device(): lax.all_gather(attend_x, 'fsdp', axis=1, tiled=True)  16.1 us
    all_gather x1, blocking collectives, per_device(): lax.all_gather(atom_weights, 'fsdp', axis=2, tiled=True)  14 us
    all_gather x1, blocking collectives, per_device(): lax.all_gather(token_to_atom, 'fsdp', axis=0, tiled=True)  12.7 us
    all_gather x1, blocking collectives, per_device(): all_rows = lax.all_gather(projected, 'seq', axis=0, tiled=True)  11.9 us
    all_gather x1, blocking collectives, token_attention(): lax.all_gather(key_rows, 'seq', axis=0, tiled=True)  11 us
    dot_general x11, matrix products, matmul(): return jnp.dot(left_side, right_side, preferred_element_type=jnp.float32)  9.49 us
  transfers between devices with their start and end apart: 4, of which 2 were waited for; matrix products, arithmetic and copies ran while one was open for 2% of the time, Pallas kernels for 0%

commit v1 on v0

v1 whole, which is shorter than its diff:
```python
import functools
import math

import jax
import jax.numpy as jnp
from jax import lax
from jax.experimental import pallas as pl
from jax.experimental.pallas import tpu as pltpu
from jax.sharding import PartitionSpec as P

HA = 4
WQ = 32
WK = 128
HD = 48
EPS = 1e-05
FAR = -1e30
RIM = (WK - WQ) // 2
VMEM_LIMIT = 56 * 1024 * 1024
MESH = pl.DeviceIdType.MESH


def layer_norm(values):
    values = values.astype(jnp.float32)
    center = values - jnp.mean(values, axis=-1, keepdims=True)
    spread = jnp.mean(center * center, axis=-1, keepdims=True)
    return center * lax.rsqrt(spread + EPS)


def matmul(left_side, right_side):
    return jnp.dot(left_side, right_side, preferred_element_type=jnp.float32)


def pack(array):
    half = array.shape[-2] // 2
    return jnp.concatenate([array[..., :half, :], array[..., half:, :]], axis=-1)


def unpack(array):
    half = array.shape[-1] // 2
    return jnp.concatenate([array[..., :half], array[..., half:]], axis=-2)


class Line:
    def __init__(self, axis, size, paired, block, out, send, recv, local, partner_send, partner_recv):
        self.axis, self.size, self.paired = axis, size, paired
        self.block, self.out, self.send, self.recv, self.local = block, out, send, recv, local
        self.partner_send, self.partner_recv = partner_send, partner_recv
        self.index = lax.axis_index(axis)
        self.stride = 2 if paired else 1
        self.length = size // self.stride
        self.position = self.index // 2 if paired else self.index
        self.parity = self.index - 2 * self.position if paired else 0

    def slot(self, position):
        return position * self.stride + self.parity

    def partner(self):
        return self.index + 1 - 2 * self.parity

    def guards(self, side, step):
        here, last = self.position, self.length - 1
        if side == 0:
            return (here - step >= 0) & (here < last), here - 1 - step >= 0
        return (here + step <= last) & (here > 0), here + 1 + step <= last

    def copy(self, side, step, arriving):
        sign = 1 if side == 0 else -1
        origin = self.position - sign * (step + (1 if arriving else 0))
        target = self.slot(self.position + sign)
        slot = self.slot(origin)
        source = self.block if (step == 0 and not arriving) else self.out.at[slot]
        return pltpu.make_async_remote_copy(
            src_ref=source,
            dst_ref=self.out.at[slot],
            send_sem=self.send.at[side, step],
            recv_sem=self.recv.at[side, step],
            device_id={self.axis: target},
            device_id_type=MESH,
        )

    def hand(self, key, origin, own, arriving):
        slot = self.slot(origin)
        landing = origin * 2 + 1 - self.parity if arriving else slot
        return pltpu.make_async_remote_copy(
            src_ref=self.block if own else self.out.at[slot],
            dst_ref=self.out.at[landing],
            send_sem=self.partner_send.at[key],
            recv_sem=self.partner_recv.at[key],
            device_id={self.axis: self.partner()},
            device_id_type=MESH,
        )

    def greet(self, barrier):
        def neighbour(target):
            pl.semaphore_signal(barrier, inc=1, device_id={self.axis: target}, device_id_type=MESH)

        expected = 0
        if self.length > 1:
            above = self.position > 0
            below = self.position < self.length - 1

            @pl.when(above)
            def _():
                neighbour(self.slot(self.position - 1))

            @pl.when(below)
            def _():
                neighbour(self.slot(self.position + 1))

            expected = jnp.where(above, 1, 0) + jnp.where(below, 1, 0)
        if self.paired:
            neighbour(self.partner())
            expected = expected + 1
        return expected

    def begin(self):
        pltpu.make_async_copy(self.block, self.out.at[self.index], self.local.at[0]).start()
        if self.paired:
            self.hand(0, self.position, True, False).start()

    def advance(self, step):
        for side in (0, 1):
            goes, unused = self.guards(side, step)
            if step > 0:
                self.arrive(side, step - 1)

            @pl.when(goes)
            def _():
                self.copy(side, step, False).start()

    def arrive(self, side, step):
        unused, comes = self.guards(side, step)

        @pl.when(comes)
        def _():
            self.copy(side, step, True).wait_recv()
            if self.paired:
                origin = self.position - (step + 1) if side == 0 else self.position + step + 1
                self.hand(1 + side * (self.length - 1) + step, origin, False, False).start()

    def steps(self):
        return self.length - 1

    def finish(self):
        last = self.length - 1
        if last > 0:
            for side in (0, 1):
                self.arrive(side, last - 1)
        for side in (0, 1):
            for step in range(last):
                goes, comes = self.guards(side, step)

                @pl.when(goes)
                def _():
                    self.copy(side, step, False).wait_send()

                if self.paired:

                    @pl.when(comes)
                    def _():
                        origin = self.position - (step + 1) if side == 0 else self.position + step + 1
                        key = 1 + side * last + step
                        self.hand(key, origin, False, False).wait_send()
                        self.hand(key, origin, False, True).wait_recv()

        if self.paired:
            self.hand(0, self.position, True, False).wait_send()
            self.hand(0, self.position, True, True).wait_recv()
        pltpu.make_async_copy(self.block, self.out.at[self.index], self.local.at[0]).wait()


class Exchange:
    def __init__(self, axis, size, block, out, send, recv, local):
        self.axis, self.size, self.block, self.out = axis, size, block, out
        self.send, self.recv, self.local = send, recv, local
        self.index = lax.axis_index(axis)

    def peer(self, shift):
        return lax.rem(self.index + shift, self.size)

    def greet(self, barrier):
        for shift in range(1, self.size):
            pl.semaphore_signal(
                barrier, inc=1, device_id={self.axis: self.peer(shift)}, device_id_type=MESH
            )
        return self.size - 1

    def copy(self, shift, arriving):
        landing = self.peer(self.size - shift) if arriving else self.index
        return pltpu.make_async_remote_copy(
            src_ref=self.block.at[self.peer(shift)],
            dst_ref=self.out.at[landing],
            send_sem=self.send.at[shift],
            recv_sem=self.recv.at[shift],
            device_id={self.axis: self.peer(shift)},
            device_id_type=MESH,
        )

    def begin(self):
        pltpu.make_async_copy(
            self.block.at[self.index], self.out.at[self.index], self.local.at[0]
        ).start()
        for shift in range(1, self.size):
            self.copy(shift, False).start()

    def steps(self):
        return 0

    def advance(self, step):
        pass

    def finish(self):
        for shift in range(1, self.size):
            self.copy(shift, False).wait_send()
            self.copy(shift, True).wait_recv()
        pltpu.make_async_copy(
            self.block.at[self.index], self.out.at[self.index], self.local.at[0]
        ).wait()


def move_kernel(kinds, *refs):
    count = len(kinds)
    blocks, outs, sems = refs[:count], refs[count : 2 * count], refs[2 * count :]
    flows, taken = [], 0
    for (kind, axis, size), block, out in zip(kinds, blocks, outs):
        if kind == "exchange":
            flows.append(Exchange(axis, size, block, out, *sems[taken : taken + 3]))
            taken += 3
        elif kind == "paired":
            flows.append(Line(axis, size, True, block, out, *sems[taken : taken + 5]))
            taken += 5
        else:
            flows.append(Line(axis, size, False, block, out, *sems[taken : taken + 3], None, None))
            taken += 3
    barrier = pltpu.get_barrier_semaphore()
    groups, seen = [], set()
    for (kind, axis, size), flow in zip(kinds, flows):
        if axis in seen:
            continue
        wide = [f for (k, a, s), f in zip(kinds, flows) if a == axis and k == "exchange"]
        groups.append(wide[0] if wide else flow)
        seen.add(axis)
    expected = 0
    for group in groups:
        expected = expected + group.greet(barrier)
    pl.semaphore_wait(barrier, expected)
    for flow in flows:
        flow.begin()
    for step in range(max(flow.steps() for flow in flows)):
        for flow in flows:
            if step < flow.steps():
                flow.advance(step)
    for flow in flows:
        flow.finish()


def move(identity, items):
    kinds, arrays, shapes, scratch = [], [], [], []
    sent = 0
    for kind, axis, array in items:
        size = lax.axis_size(axis)
        kinds.append((kind, axis, size))
        arrays.append(array)
        shape = array.shape if kind == "exchange" else (size,) + array.shape
        shapes.append(jax.ShapeDtypeStruct(shape, array.dtype))
        sent += array.size * array.dtype.itemsize
        dma = pltpu.SemaphoreType.DMA
        if kind == "exchange":
            scratch += [dma((size,)), dma((size,)), dma((1,))]
        else:
            length = size // 2 if kind == "paired" else size
            steps = max(length - 1, 1)
            scratch += [dma((2, steps)), dma((2, steps)), dma((1,))]
            if kind == "paired":
                scratch += [dma((2 * length,)), dma((2 * length,))]
    return pl.pallas_call(
        functools.partial(move_kernel, tuple(kinds)),
        out_shape=tuple(shapes),
        in_specs=[pl.BlockSpec(memory_space=pltpu.VMEM)] * len(arrays),
        out_specs=tuple([pl.BlockSpec(memory_space=pltpu.VMEM)] * len(arrays)),
        scratch_shapes=scratch,
        compiler_params=pltpu.CompilerParams(
            collective_id=identity, has_side_effects=True, vmem_limit_bytes=VMEM_LIMIT
        ),
        cost_estimate=pl.CostEstimate(flops=0, bytes_accessed=30 * sent, transcendentals=0),
        name=f"move{identity}",
    )(*arrays)


def attention_kernel(heads, span, q_ref, gate_ref, kv_ref, bias_ref, mask_ref, out_ref):
    rows, width = q_ref.shape[1], q_ref.shape[2]
    pieces, piece_rows = kv_ref.shape[0], kv_ref.shape[2]
    queries = q_ref[0]
    head_of = lax.broadcasted_iota(jnp.int32, (rows, width), 1) // HD
    stacked = jnp.concatenate(
        [jnp.where(head_of == head, queries, 0).astype(jnp.bfloat16) for head in range(heads)], axis=0
    )
    scale = 1.0 / math.sqrt(HD)
    maxima = totals = summed = None
    for first in range(0, pieces, span):
        taken = min(span, pieces - first)
        keys = jnp.concatenate([kv_ref[first + i, 0, :, :width] for i in range(taken)], axis=0)
        values = jnp.concatenate([kv_ref[first + i, 0, :, width:] for i in range(taken)], axis=0)
        columns = pl.ds(first * piece_rows, taken * piece_rows)
        scores = (
            lax.dot_general(
                stacked, keys, (((1,), (1,)), ((), ())), preferred_element_type=jnp.float32
            )
            * scale
        )
        bias = bias_ref[:, :, columns].reshape(heads * rows, taken * piece_rows)
        scores = scores + bias.astype(jnp.float32)
        scores = jnp.where(mask_ref[:, columns] > 0, scores, FAR)
        block_max = jnp.max(scores, axis=-1, keepdims=True)
        new_maxima = block_max if maxima is None else jnp.maximum(maxima, block_max)
        weights = jnp.exp(scores - new_maxima)
        block_total = jnp.sum(weights, axis=-1, keepdims=True)
        update = matmul(weights.astype(jnp.bfloat16), values)
        if maxima is None:
            totals, summed = block_total, update
        else:
            factor = jnp.exp(maxima - new_maxima)
            totals = totals * factor + block_total
            summed = summed * factor + update
        maxima = new_maxima
    attended = summed / totals
    result = jnp.zeros((rows, width), jnp.float32)
    for head in range(heads):
        result = result + jnp.where(head_of == head, attended[head * rows : (head + 1) * rows], 0.0)
    gate = jax.nn.sigmoid(gate_ref[0].astype(jnp.float32))
    out_ref[0] = (result * gate).astype(jnp.bfloat16)


def token_attention(query_rows, gate_rows, kv_all, pair_bias, mask_row):
    groups, rows, width = query_rows.shape
    heads, keys = pair_bias.shape[0], pair_bias.shape[2]
    pieces, piece_rows = kv_all.shape[0], kv_all.shape[2]
    one = lambda g: (g, 0, 0)
    return pl.pallas_call(
        functools.partial(attention_kernel, heads, max(512 // piece_rows, 1)),
        grid=(groups,),
        in_specs=[
            pl.BlockSpec((1, rows, width), one),
            pl.BlockSpec((1, rows, width), one),
            pl.BlockSpec((pieces, 1, piece_rows, 2 * width), lambda g: (0, g, 0, 0)),
            pl.BlockSpec((heads, rows, keys), lambda g: (0, 0, 0)),
            pl.BlockSpec((1, keys), lambda g: (0, 0)),
        ],
        out_specs=pl.BlockSpec((1, rows, width), one),
        out_shape=jax.ShapeDtypeStruct((groups, rows, width), jnp.bfloat16),
        compiler_params=pltpu.CompilerParams(vmem_limit_bytes=VMEM_LIMIT),
        name="token_attention",
    )(query_rows, gate_rows, kv_all, pair_bias, mask_row)


def atom_kernel(
    first_ref, bounds_ref, rows_ref, skip_ref, cond_ref, token_ref, weight_ref, vector_ref,
    position_ref, bias_ref, out_ref, state_ref, query_ref, gate_ref, key_ref, value_ref, held_ref,
):
    count, channels = query_ref.shape
    head_width = channels // HA
    tokens = rows_ref.shape[0]
    chunk = min(512, tokens)
    inner = pl.ds(RIM, count)
    owners = token_ref[...]
    taken = jnp.zeros((owners.shape[0], channels), jnp.float32)
    for start in range(0, tokens, chunk):
        column = lax.broadcasted_iota(jnp.int32, (owners.shape[0], chunk), 1) + start
        hit = jnp.where(owners == column, 1.0, 0.0).astype(jnp.bfloat16)
        taken = taken + matmul(hit, rows_ref[start : start + chunk, :])
    state = skip_ref[...].astype(jnp.float32) + taken
    state_ref[...] = state
    normed = layer_norm(cond_ref[...]).astype(jnp.bfloat16)
    atom_x = (
        jax.nn.sigmoid(matmul(normed, weight_ref[0]) + vector_ref[0:1, :]) * layer_norm(state)
        + matmul(normed, weight_ref[1])
    ).astype(jnp.bfloat16)
    own_x = atom_x[RIM : RIM + count, :]
    query_ref[...] = (matmul(own_x, weight_ref[2]) + vector_ref[1:2, :]).astype(jnp.bfloat16)
    gate_ref[...] = matmul(own_x, weight_ref[5]).astype(jnp.bfloat16)
    key_ref[...] = matmul(atom_x, weight_ref[3]).astype(jnp.bfloat16)
    value_ref[...] = matmul(atom_x, weight_ref[4]).astype(jnp.bfloat16)
    head_of = lax.broadcasted_iota(jnp.int32, (WQ, channels), 1) // head_width
    lane = lax.broadcasted_iota(jnp.int32, (1, WK), 1)
    scale = 1.0 / math.sqrt(head_width)

    def window(index, carry):
        base = pl.multiple_of(index * WQ, WQ)
        queries = query_ref[pl.ds(base, WQ), :]
        stacked = jnp.concatenate(
            [jnp.where(head_of == head, queries, 0).astype(jnp.bfloat16) for head in range(HA)], axis=0
        )
        keys = key_ref[pl.ds(base, WK), :]
        values = value_ref[pl.ds(base, WK), :]
        scores = (
            lax.dot_general(
                stacked, keys, (((1,), (1,)), ((), ())), preferred_element_type=jnp.float32
            )
            * scale
        )
        scores = scores + bias_ref[:, pl.ds(base, WQ), :].reshape(HA * WQ, WK).astype(jnp.float32)
        slot = first_ref[0] + base - RIM + lane
        inside = (slot >= bounds_ref[2 * index]) & (slot < bounds_ref[2 * index + 1])
        scores = jnp.where(inside, scores, FAR)
        weights = jnp.exp(scores - jnp.max(scores, axis=-1, keepdims=True))
        totals = jnp.sum(weights, axis=-1, keepdims=True)
        attended = matmul(weights.astype(jnp.bfloat16), values) / totals
        result = jnp.zeros((WQ, channels), jnp.float32)
        for head in range(HA):
            result = result + jnp.where(head_of == head, attended[head * WQ : (head + 1) * WQ], 0.0)
        held_ref[pl.ds(base, WQ), :] = result
        return carry

    lax.fori_loop(0, count // WQ, window, 0, unroll=UNROLL)
    gated = (held_ref[...] * jax.nn.sigmoid(gate_ref[...].astype(jnp.float32))).astype(jnp.bfloat16)
    fresh = state_ref[inner, :] + matmul(gated, weight_ref[6])
    final = layer_norm(fresh).astype(jnp.bfloat16)
    out_ref[...] = lax.dot_general(
        position_ref[...], final, (((1,), (1,)), ((), ())), preferred_element_type=jnp.float32
    )


UNROLL = 8


def atom_block(first, bounds, rows, skip, cond, owners, weights, vectors, positions, bias):
    count, channels = bias.shape[1], skip.shape[1]
    extended = skip.shape[0]
    smem = pl.BlockSpec(memory_space=pltpu.SMEM)
    vmem = pl.BlockSpec(memory_space=pltpu.VMEM)
    return pl.pallas_call(
        atom_kernel,
        in_specs=[smem, smem] + [vmem] * 8,
        out_specs=vmem,
        out_shape=jax.ShapeDtypeStruct((positions.shape[0], count), jnp.float32),
        scratch_shapes=[
            pltpu.VMEM((extended, channels), jnp.float32),
            pltpu.VMEM((count, channels), jnp.bfloat16),
            pltpu.VMEM((count, channels), jnp.bfloat16),
            pltpu.VMEM((extended, channels), jnp.bfloat16),
            pltpu.VMEM((extended, channels), jnp.bfloat16),
            pltpu.VMEM((count, channels), jnp.float32),
        ],
        compiler_params=pltpu.CompilerParams(vmem_limit_bytes=VMEM_LIMIT),
        name="atom_block",
    )(first, bounds, rows, skip, cond, owners, weights, vectors, positions, bias)


def rim_extended(array, axis):
    size, length = (lax.axis_size(axis), array.shape[0])
    up = [(i, (i + 1) % size) for i in range(size - 1)]
    down = [(j, i) for i, j in up]
    before = lax.ppermute(array[length - RIM :], axis, up)
    after = lax.ppermute(array[:RIM], axis, down)
    return jnp.concatenate([before, array, after], axis=0)


def per_device(
    token_act,
    token_cond,
    pair_bias,
    token_mask,
    ada_weights,
    attention_in,
    attention_out,
    transition_in,
    transition_out,
    token_vectors,
    atom_skip,
    atom_cond,
    atom_bias,
    window_bounds,
    atom_token,
    atom_weights,
    token_to_atom,
    atom_vectors,
    position_out,
):
    groups = lax.axis_size("fsdp")
    act_rows = token_act[0]
    row_count, depth = act_rows.shape
    column_count = attention_in.shape[2]
    channels = atom_cond.shape[1]
    start = lax.axis_index("fsdp") * column_count
    atom_pair = rim_extended(jnp.concatenate([atom_skip[0], atom_cond], axis=1), "seq")
    owners = rim_extended(atom_token, "seq")[:, None]

    cond_normed = layer_norm(token_cond[0]).astype(jnp.bfloat16)
    act_normed = layer_norm(act_rows).astype(jnp.bfloat16)
    act_slots = jnp.transpose(act_normed.reshape(row_count, groups, column_count), (1, 0, 2))
    cond_all, act_all, mask_all = move(
        1,
        (
            ("line", "fsdp", cond_normed),
            ("exchange", "fsdp", pack(act_slots)),
            ("paired", "seq", token_mask[None]),
        ),
    )
    cond_flat = cond_all.reshape(groups * row_count, depth)
    act_flat = unpack(act_all).reshape(groups * row_count, column_count).astype(jnp.float32)

    def adaptive(scale_index, shift_index, vector_index):
        offset = lax.dynamic_slice_in_dim(token_vectors[vector_index], start, column_count)
        scaled = jax.nn.sigmoid(matmul(cond_flat, ada_weights[scale_index]) + offset) * act_flat
        rows = (scaled + matmul(cond_flat, ada_weights[shift_index])).astype(jnp.bfloat16)
        return pack(rows.reshape(groups, row_count, column_count))

    def joined(array):
        array = unpack(array)
        return jnp.transpose(array, (1, 2, 0, 3)).reshape(groups * row_count, depth)

    (attend_all,) = move(2, (("line", "fsdp", adaptive(0, 1, 0)),))
    transit_part = adaptive(2, 3, 1)
    attend_flat = joined(attend_all)
    query_bias = lax.dynamic_slice_in_dim(token_vectors[2], start, column_count)

    def project(index):
        return matmul(attend_flat, attention_in[index])

    def grouped(array):
        return array.astype(jnp.bfloat16).reshape(groups, row_count, -1)

    keys_values = jnp.concatenate([grouped(project(1)), grouped(project(2))], axis=-1)
    kv_all, transit_all, small_all = move(
        3,
        (
            ("paired", "seq", keys_values),
            ("line", "fsdp", transit_part),
            (
                "line",
                "fsdp",
                jnp.concatenate(
                    [
                        atom_weights.reshape(-1, channels),
                        token_to_atom,
                    ],
                    axis=0,
                ),
            ),
        ),
    )
    query_rows = grouped(project(0) + query_bias)
    gate_rows = grouped(project(3))
    weight_rows = atom_weights.size // channels
    atom_full = jnp.transpose(
        small_all[:, :weight_rows].reshape((groups,) + atom_weights.shape), (1, 2, 0, 3)
    ).reshape(atom_weights.shape[0], channels, channels)
    project_full = small_all[:, weight_rows:].reshape(depth, channels)
    gated = token_attention(
        query_rows, gate_rows, kv_all, pair_bias, mask_all.reshape(1, -1)
    ).reshape(groups * row_count, -1)
    transit_flat = joined(transit_all)
    hidden = (
        jax.nn.silu(matmul(transit_flat, transition_in[0])) * matmul(transit_flat, transition_in[1])
    ).astype(jnp.bfloat16)
    partial_sum = matmul(gated, attention_out) + matmul(hidden, transition_out)
    (parts,) = move(
        4,
        (("exchange", "fsdp", partial_sum.astype(jnp.bfloat16).reshape(groups, row_count, depth)),),
    )
    combined = jnp.sum(parts.astype(jnp.float32), axis=0)
    token_result = (act_rows.astype(jnp.float32) + combined).astype(jnp.bfloat16)
    projected = matmul(token_result, project_full).astype(jnp.bfloat16)
    (all_rows,) = move(5, (("paired", "seq", projected),))
    first_atom = (lax.axis_index("seq") * atom_cond.shape[0]).astype(jnp.int32).reshape(1)
    update = atom_block(
        first_atom,
        window_bounds.reshape(-1),
        all_rows.reshape(-1, channels),
        atom_pair[:, :channels],
        atom_pair[:, channels:],
        owners,
        atom_full,
        atom_vectors,
        position_out,
        atom_bias,
    )
    return (token_result[None], update[None])


def solution(mesh):
    in_specs = (
        P(("sample", "fsdp"), "seq", None),
        P(("sample", "fsdp"), "seq", None),
        P("fsdp", "seq", None),
        P("seq"),
        P(None, None, "fsdp"),
        P(None, None, "fsdp"),
        P("fsdp", None),
        P(None, None, "fsdp"),
        P("fsdp", None),
        P(),
        P(("sample", "fsdp"), "seq", None),
        P("seq", None),
        P(None, "seq", None),
        P("seq", None),
        P("seq"),
        P(None, None, "fsdp"),
        P("fsdp", None),
        P(),
        P(),
    )
    out_specs = (P(("sample", "fsdp"), "seq", None), P(("sample", "fsdp"), None, "seq"))
    return jax.shard_map(
        per_device, mesh=mesh, in_specs=in_specs, out_specs=out_specs, check_vma=False
    )
```

time: 256 us -> 171 us (0.67)
  Pallas kernels: 0 us -> 117 us
  blocking collectives: 96.4 us -> 0 us
  waiting for transfers between devices: 86.8 us -> 0.01 us
  matrix products: 29.8 us -> 15 us
  between operations: 14.6 us -> 1.25 us
  starting transfers between devices: 4.4 us -> 10.7 us
    pallas_call x0 -> x7, Pallas kernels: none -> 117 us  [the longest x5 98.5 us: move(): pl.pallas_call(functools.partial(move_kernel, tuple(kinds)), out_shape=tu...]
    all_gather x8 -> x0, blocking collectives: 96.4 us -> none  [the longest x1 16.2 us: per_device(): lax.all_gather(transit_x, 'fsdp', axis=1, tiled=True)]
    all_gather x1 -> x0, waiting for transfers between devices: 85 us -> none  [per_device(): lax.all_gather(ada_weights, 'fsdp', axis=2, tiled=True)]
    dot_general x10 -> x0, matrix products: 16.6 us -> none  [the longest x1 3.87 us: per_device(): jnp.einsum('tsf,fd->tsd', hidden, transition_out, preferred_element_type=...]
    ppermute x2 -> x4, starting transfers between devices: 4.33 us -> 10.7 us  [the longest x2 6.91 us: rim_extended(): before = lax.ppermute(array[length - RIM:], axis, up)]
    dot_general x11 -> x12, matrix products: 9.49 us -> 15 us  [matmul(): return jnp.dot(left_side, right_side, preferred_element_type=jnp.float32)]
    sub x1 -> x0, matrix products: 3.7 us -> none  [window_attention(): weights = jnp.exp(scores - maxima)]
    convert_element_type x0 -> x9, local copies, waits for them, and re-layouts: none -> 3.63 us  [the longest x4 1.93 us: grouped(): return array.astype(jnp.bfloat16).reshape(groups, row_count, -1)]
  transfers between devices with their start and end apart: 4 -> 4, of which waited for: 2 -> 0; matrix products, arithmetic and copies ran while one was open for 2% -> 21% of each run, Pallas kernels for 0% -> 62%
where the time goes in v1:
time: 171 us; the launch traced here: 169 us
  Pallas kernels  117 us (68%)
  local copies, waits for them, and re-layouts  16.8 us (10%)
  matrix products  15 us (9%)
  starting transfers between devices  10.7 us (6%)
  other arithmetic  8.27 us (5%)
    pallas_call x5, Pallas kernels, move(): pl.pallas_call(functools.partial(move_kernel, tuple(kinds)), out_shape=tu...  98.5 us
    dot_general x12, matrix products, matmul(): return jnp.dot(left_side, right_side, preferred_element_type=jnp.float32)  15 us
    pallas_call x1, Pallas kernels, atom_block(): pl.pallas_call(atom_kernel, in_specs=[smem, smem] + [vmem] * 8, out_specs...  12.4 us
    ppermute x2, starting transfers between devices, rim_extended(): before = lax.ppermute(array[length - RIM:], axis, up)  6.91 us
    pallas_call x1, Pallas kernels, token_attention(): pl.pallas_call(functools.partial(attention_kernel, heads, max(512 // piec...  5.7 us
    slice x3, local copies, waits for them, and re-layouts, unpack(): return jnp.concatenate([array[..., :half], array[..., half:]], axis=-2)  4.04 us
    ppermute x2, starting transfers between devices, rim_extended(): after = lax.ppermute(array[:RIM], axis, down)  3.83 us
  transfers between devices with their start and end apart: 4, of which 0 were waited for; matrix products, arithmetic and copies ran while one was open for 21% of the time, Pallas kernels for 62%

profile of v1, /device:TPU:1, one launch (start us, length us, event | category | flops | bytes accessed | tf_op | source)
XLA Modules:
  0.0 168.7 jit_solution(12991332122960870240)
XLA Ops:
  1.5 1.9 %collective-permute-start.1 = (bf16[48,256]{1,0:T(8,128)(2,1)S(1)}, bf16[48,256]{1,0:T(8,128)(2,1)S(1)}, u32[]{:S(2)}, u32[]{:S(2)}) collective-permute-start(bf16[48,256]{1,0:T(8,128)(2,1)S(1)} %get-tuple-element.29), channel_id=1, source_target_pairs={{1,0},{2,1},{3,2},{5,4},{6,5},{7,6},{9,8},{10,9},{11,10},{13,12},{... | collective-permute-start | bytes 73736 | tf_op jit(solution)/shard_map/ppermute | solution.py:454
  3.4 4.5 %collective-permute-start = (bf16[48,256]{1,0:T(8,128)(2,1)S(1)}, bf16[48,256]{1,0:T(8,128)(2,1)S(1)}, u32[]{:S(2)}, u32[]{:S(2)}) collective-permute-start(bf16[48,256]{1,0:T(8,128)(2,1)S(1)} %get-tuple-element.28), channel_id=1, source_target_pairs={{0,1},{1,2},{2,3},{4,5},{5,6},{6,7},{8,9},{9,10},{10,11},{12,13},{... | collective-permute-start | bytes 73736 | tf_op jit(solution)/shard_map/ppermute | solution.py:453
  8.8 2.4 %collective-permute-start.2 = (s32[48]{0:T(128)S(1)}, s32[48]{0:T(128)S(1)}, u32[]{:S(2)}, u32[]{:S(2)}) collective-permute-start(s32[48]{0:T(128)S(1)} %get-tuple-element.42), channel_id=1, source_target_pairs={{0,1},{1,2},{2,3},{4,5},{5,6},{6,7},{8,9},{9,10},{10,11},{12,13},{... | collective-permute-start | bytes 584 | tf_op jit(solution)/shard_map/ppermute | solution.py:453
  11.2 1.9 %collective-permute-start.3 = (s32[48]{0:T(128)S(1)}, s32[48]{0:T(128)S(1)}, u32[]{:S(2)}, u32[]{:S(2)}) collective-permute-start(s32[48]{0:T(128)S(1)} %get-tuple-element.41), channel_id=1, source_target_pairs={{1,0},{2,1},{3,2},{5,4},{6,5},{7,6},{9,8},{10,9},{11,10},{13,12},{... | collective-permute-start | bytes 584 | tf_op jit(solution)/shard_map/ppermute | solution.py:454
  16.9 28.8 %move1.1 = (bf16[4,128,768]{2,1,0:T(8,128)(2,1)}, bf16[4,64,384]{2,1,0:T(8,128)(2,1)}, s32[4,1,128]{2,1,0:T(1,128)}) custom-call(bf16[128,768]{1,0:T(8,128)(2,1)} %fusion.44.refs_0_, bf16[4,64,384]{2,1,0:T(8,128)(2,1)} %pad_maximum_fusion.3.refs_1_, s32[1,128]{1,0:T(1,128)} %bitcast.148), custom_call_target="tpu_custom_call" | custom-call | bytes 11811840 | tf_op jit(solution)/shard_map/move1/pallas_call | solution.py:276
  45.7 1.1 fusion.74
  47.9 1.4 fusion.10
  49.3 1.4 fusion.11
  51.7 17.8 %move2.1 = bf16[4,4,64,384]{3,2,1,0:T(8,128)(2,1)} custom-call(bf16[4,64,384]{2,1,0:T(8,128)(2,1)} %pad_maximum_fusion.4.refs_0_), custom_call_target="tpu_custom_call" | custom-call | bytes 5898240 | tf_op jit(solution)/shard_map/move2/pallas_call | solution.py:276
  69.5 1.5 fusion.69
  71.8 1.4 convolution_convert_fusion.2
  76.3 1.4 fusion.5
  77.8 1.4 fusion.12
  82.0 25.7 %move3.1 = (bf16[4,4,128,384]{3,2,1,0:T(8,128)(2,1)}, bf16[4,4,64,384]{3,2,1,0:T(8,128)(2,1)}, bf16[4,416,128]{2,1,0:T(8,128)(2,1)}) custom-call(bf16[4,128,384]{2,1,0:T(8,128)(2,1)} %pad_maximum_fusion.1.refs_0_, bf16[4,64,384]{2,1,0:T(8,128)(2,1)} %pad_maximum_fusion.5.refs_1_, bf16[416,128]{1,0:T(8,128)(2,1)} %pad_maximum_fusion.6.refs_2_), custom_call_target="tpu_custom_call" | custom-call | bytes 20889600 | tf_op jit(solution)/shard_map/move3/pallas_call | solution.py:276
  107.8 1.5 fusion.68
  110.1 5.7 %token_attention.1 = bf16[4,128,192]{2,1,0:T(8,128)(2,1)} custom-call(bf16[4,128,192]{2,1,0:T(8,128)(2,1)} %bitcast.124, bf16[4,128,192]{2,1,0:T(8,128)(2,1)} %bitcast.125, bf16[4,4,128,384]{3,2,1,0:T(8,128)(2,1)} %get-tuple-element.10.kv_ref, bf16[4,128,512]{2,1,0:T(8,128)(2,1)} %bias_ref.2, s32[1,512]{1,0:T(1,128)} %bitcast.144), custom_call_target="tpu_custom_call" | custom-call | tf_op jit(solution)/shard_map/token_attention/pallas_call | solution.py:339
  115.8 1.4 fusion.77
  117.2 1.5 fusion.16
  118.7 3.3 %add_convert_fusion = bf16[512,768]{1,0:T(8,128)(2,1)} fusion(f32[512,768]{1,0:T(8,128)S(1)} %fusion.77, bf16[384,768]{1,0:T(8,128)(2,1)S(1)} %copy-done, f32[512,384]{1,0:T(8,128)} %fusion.16, bf16[96,8,4,128]{3,2,1,0:T(4,128)(2,1)S(1)} %bitcast.139, bf16[2,768,384]{2,1,0:T(8,128)(2,1)} %param.26), kind=kOutput, calls=%fused_computation.1 | convolution fusion | flops 605945856 | bytes 5111808 | tf_op jit(solution)/shard_map/dot_general | solution.py:30
  122.1 17.7 %move4.1 = bf16[4,128,768]{2,1,0:T(8,128)(2,1)} custom-call(bf16[4,128,768]{2,1,0:T(8,128)(2,1)} %bitcast.140), custom_call_target="tpu_custom_call" | custom-call | bytes 23592960 | tf_op jit(solution)/shard_map/move4/pallas_call | solution.py:276
  139.7 1.3 convert_reduce_fusion
  142.8 8.5 %move5.1 = bf16[4,128,128]{2,1,0:T(8,128)(2,1)} custom-call(bf16[128,128]{1,0:T(8,128)(2,1)} %convolution_convert_fusion.3.refs_0_), custom_call_target="tpu_custom_call" | custom-call | bytes 983040 | tf_op jit(solution)/shard_map/move5/pallas_call | solution.py:276
  154.9 12.4 %atom_block.1 = f32[3,1024]{1,0:T(4,128)} custom-call(s32[1]{0:T(128)} %bitcast.33.first_ref, s32[64]{0:T(128)} %reshape.127.bounds_ref, bf16[512,128]{1,0:T(8,128)(2,1)} %bitcast.142, bf16[1120,128]{1,0:T(8,128)(2,1)} %get-tuple-element.27.skip_ref, bf16[1120,128]{1,0:T(8,128)(2,1)} %get-tuple-element.26.cond_ref, s32[1120,1]{1,0:T(8,128)} %broadcast_in_dim.9.token_ref, ...), custom_call_target="tpu_custom_call" | custom-call | tf_op jit(solution)/shard_map/atom_block/pallas_call | solution.py:431
  167.3 1.3 copy.88
  (96 shorter events, 20.2 us)
Async XLA Ops:
  0.6 118.1 %copy-start = (bf16[384,768]{1,0:T(8,128)(2,1)S(1)}, bf16[384,768]{1,0:T(8,128)(2,1)}, u32[]{:S(2)}) copy-start(bf16[384,768]{1,0:T(8,128)(2,1)} %param.27) | copy-start | bytes 1769476
  0.6 13.6 %copy-start.2 = (bf16[1,128,768]{2,1,0:T(8,128)(2,1)S(1)}, bf16[1,128,768]{2,1,0:T(8,128)(2,1)}, u32[]{:S(2)}) copy-start(bf16[1,128,768]{2,1,0:T(8,128)(2,1)} %param.19) | copy-start | bytes 589828
  0.7 13.7 %copy-start.3 = (bf16[1,128,768]{2,1,0:T(8,128)(2,1)S(1)}, bf16[1,128,768]{2,1,0:T(8,128)(2,1)}, u32[]{:S(2)}) copy-start(bf16[1,128,768]{2,1,0:T(8,128)(2,1)} %param.20) | copy-start | bytes 589828
  1.5 152.5 %collective-permute-start.1 = (bf16[48,256]{1,0:T(8,128)(2,1)S(1)}, bf16[48,256]{1,0:T(8,128)(2,1)S(1)}, u32[]{:S(2)}, u32[]{:S(2)}) collective-permute-start(bf16[48,256]{1,0:T(8,128)(2,1)S(1)} %get-tuple-element.29), channel_id=1, source_target_pairs={{1,0},{2,1},{3,2},{5,4},{6,5},{7,6},{9,8},{10,9},{11,10},{13,12},{... | collective-permute-start | bytes 73736 | tf_op jit(solution)/shard_map/ppermute | solution.py:454
  3.4 150.6 %collective-permute-start = (bf16[48,256]{1,0:T(8,128)(2,1)S(1)}, bf16[48,256]{1,0:T(8,128)(2,1)S(1)}, u32[]{:S(2)}, u32[]{:S(2)}) collective-permute-start(bf16[48,256]{1,0:T(8,128)(2,1)S(1)} %get-tuple-element.28), channel_id=1, source_target_pairs={{0,1},{1,2},{2,3},{4,5},{5,6},{6,7},{8,9},{9,10},{10,11},{12,13},{... | collective-permute-start | bytes 73736 | tf_op jit(solution)/shard_map/ppermute | solution.py:453
  8.8 144.1 %collective-permute-start.2 = (s32[48]{0:T(128)S(1)}, s32[48]{0:T(128)S(1)}, u32[]{:S(2)}, u32[]{:S(2)}) collective-permute-start(s32[48]{0:T(128)S(1)} %get-tuple-element.42), channel_id=1, source_target_pairs={{0,1},{1,2},{2,3},{4,5},{5,6},{6,7},{8,9},{9,10},{10,11},{12,13},{... | collective-permute-start | bytes 584 | tf_op jit(solution)/shard_map/ppermute | solution.py:453
  11.2 141.7 %collective-permute-start.3 = (s32[48]{0:T(128)S(1)}, s32[48]{0:T(128)S(1)}, u32[]{:S(2)}, u32[]{:S(2)}) collective-permute-start(s32[48]{0:T(128)S(1)} %get-tuple-element.41), channel_id=1, source_target_pairs={{1,0},{2,1},{3,2},{5,4},{6,5},{7,6},{9,8},{10,9},{11,10},{13,12},{... | collective-permute-start | bytes 584 | tf_op jit(solution)/shard_map/ppermute | solution.py:454
  46.7 0.7 copy-start.13
  46.8 1.1 copy-start.1
  47.5 1.9 %copy-start.8 = (f32[512,192]{0,1:T(8,128)}, f32[512,192]{0,1:T(8,128)S(1)}, u32[]{:S(2)}) copy-start(f32[512,192]{0,1:T(8,128)S(1)} %copy.73) | copy-start | bytes 1179652
  71.8 1.4 copy-start.16
  74.3 2.0 %copy-start.9 = (f32[512,192]{0,1:T(8,128)S(1)}, f32[512,192]{0,1:T(8,128)}, u32[]{:S(2)}) copy-start(f32[512,192]{0,1:T(8,128)} %copy-done.8) | copy-start | bytes 1179652
  77.8 1.6 copy-start.11
  79.3 2.1 %copy-start.12 = (bf16[192,128]{1,0:T(8,128)(2,1)S(1)}, bf16[192,128]{1,0:T(8,128)(2,1)}, u32[]{:S(2)}) copy-start(bf16[192,128]{1,0:T(8,128)(2,1)} %param.35) | copy-start | bytes 147460
  110.1 5.7 %copy-start.10 = (bf16[192,768]{1,0:T(8,128)(2,1)S(1)}, bf16[192,768]{1,0:T(8,128)(2,1)}, u32[]{:S(2)}) copy-start(bf16[192,768]{1,0:T(8,128)(2,1)} %param.25) | copy-start | bytes 884740
  115.8 1.4 copy-start.17
  139.7 1.4 copy-start.7
  141.1 0.9 copy-start.15
  141.1 10.6 %copy-start.6 = (bf16[1,128,768]{2,1,0:T(8,128)(2,1)}, bf16[1,128,768]{2,1,0:T(8,128)(2,1)S(1)}, u32[]{:S(2)}) copy-start(bf16[1,128,768]{2,1,0:T(8,128)(2,1)S(1)} %fusion.45) | copy-start | bytes 589828
  151.3 1.6 copy-start.14
  151.7 2.3 %copy-start.4 = (bf16[1024,128]{1,0:T(8,128)(2,1)S(1)}, bf16[1024,128]{1,0:T(8,128)(2,1)}, u32[]{:S(2)}) copy-start(bf16[1024,128]{1,0:T(8,128)(2,1)} %param.30) | copy-start | bytes 786436
  151.7 2.3 %copy-start.5 = (bf16[1,1024,128]{2,1,0:T(8,128)(2,1)S(1)}, bf16[1,1024,128]{2,1,0:T(8,128)(2,1)}, u32[]{:S(2)}) copy-start(bf16[1,1024,128]{2,1,0:T(8,128)(2,1)} %param.29) | copy-start | bytes 786436

commit v2 on v1

--- a/solution.py
+++ b/solution.py
@@ -218,32 +218,98 @@
         ).wait()
 
 
-def move_kernel(kinds, *refs):
-    count = len(kinds)
-    blocks, outs, sems = refs[:count], refs[count : 2 * count], refs[2 * count :]
-    flows, taken = [], 0
-    for (kind, axis, size), block, out in zip(kinds, blocks, outs):
-        if kind == "exchange":
-            flows.append(Exchange(axis, size, block, out, *sems[taken : taken + 3]))
-            taken += 3
-        elif kind == "paired":
-            flows.append(Line(axis, size, True, block, out, *sems[taken : taken + 5]))
-            taken += 5
-        else:
-            flows.append(Line(axis, size, False, block, out, *sems[taken : taken + 3], None, None))
-            taken += 3
-    barrier = pltpu.get_barrier_semaphore()
-    groups, seen = [], set()
-    for (kind, axis, size), flow in zip(kinds, flows):
-        if axis in seen:
-            continue
-        wide = [f for (k, a, s), f in zip(kinds, flows) if a == axis and k == "exchange"]
-        groups.append(wide[0] if wide else flow)
-        seen.add(axis)
-    expected = 0
-    for group in groups:
-        expected = expected + group.greet(barrier)
-    pl.semaphore_wait(barrier, expected)
+class Halo:
+    def __init__(self, axis, size, block, out, send, recv):
+        self.axis, self.size, self.block, self.out = axis, size, block, out
+        self.send, self.recv = send, recv
+        self.index = lax.axis_index(axis)
+        self.above, self.below = self.index > 0, self.index < size - 1
+
+    def greet(self, barrier):
+        for present, target in ((self.above, self.index - 1), (self.below, self.index + 1)):
+
+            @pl.when(present)
+            def _():
+                pl.semaphore_signal(
+                    barrier, inc=1, device_id={self.axis: target}, device_id_type=MESH
+                )
+
+        return jnp.where(self.above, 1, 0) + jnp.where(self.below, 1, 0)
+
+    def copy(self, side):
+        return pltpu.make_async_remote_copy(
+            src_ref=self.block.at[side],
+            dst_ref=self.out.at[1 - side],
+            send_sem=self.send.at[side],
+            recv_sem=self.recv.at[side],
+            device_id={self.axis: self.index - 1 + 2 * side},
+            device_id_type=MESH,
+        )
+
+    def begin(self):
+        for side, present in ((0, self.above), (1, self.below)):
+
+            @pl.when(present)
+            def _():
+                self.copy(side).start()
+
+            @pl.when(jnp.logical_not(present))
+            def _():
+                self.out[side] = jnp.zeros(self.out.shape[1:], self.out.dtype)
+
+    def steps(self):
+        return 0
+
+    def finish(self):
+        for side, present in ((0, self.above), (1, self.below)):
+
+            @pl.when(present)
+            def _():
+                self.copy(side).wait_send()
+                self.copy(1 - side).wait_recv()
+
+
+class Swap:
+    def __init__(self, axis, size, block, out, send, recv, local):
+        self.axis, self.block, self.out = axis, block, out
+        self.send, self.recv, self.local = send, recv, local
+        self.index = lax.axis_index(axis)
+        self.parity = lax.rem(self.index, 2)
+
+    def copy(self, arriving):
+        return pltpu.make_async_remote_copy(
+            src_ref=self.block,
+            dst_ref=self.out.at[1 - self.parity if arriving else self.parity],
+            send_sem=self.send.at[0],
+            recv_sem=self.recv.at[0],
+            device_id={self.axis: self.index + 1 - 2 * self.parity},
+            device_id_type=MESH,
+        )
+
+    def begin(self):
+        pltpu.make_async_copy(self.block, self.out.at[self.parity], self.local.at[0]).start()
+        self.copy(False).start()
+
+    def steps(self):
+        return 0
+
+    def finish(self):
+        self.copy(False).wait_send()
+        self.copy(True).wait_recv()
+        pltpu.make_async_copy(self.block, self.out.at[self.parity], self.local.at[0]).wait()
+
+
+def line_scratch(size, paired):
+    dma = pltpu.SemaphoreType.DMA
+    length = size // 2 if paired else size
+    steps = max(length - 1, 1)
+    scratch = [dma((2, steps)), dma((2, steps)), dma((1,))]
+    if paired:
+        scratch += [dma((2 * length,)), dma((2 * length,))]
+    return scratch
+
+
+def run_flows(flows):
     for flow in flows:
         flow.begin()
     for step in range(max(flow.steps() for flow in flows)):
@@ -254,25 +320,75 @@
         flow.finish()
 
 
+def move_kernel(kinds, *refs):
+    count = len(kinds)
+    blocks, outs, sems = refs[:count], refs[count : 2 * count], list(refs[2 * count :])
+    flows, leaders = [], {}
+
+    def take(number):
+        taken = sems[:number]
+        del sems[:number]
+        return taken
+
+    for (kind, axis, size, chunks), block, out in zip(kinds, blocks, outs):
+        if kind == "exchange":
+            flow = Exchange(axis, size, block, out, *take(3))
+            leaders[axis] = flow
+            flows.append(flow)
+        elif kind == "halo":
+            flows.append(Halo(axis, size, block, out, *take(2)))
+        elif kind == "swap":
+            flows.append(Swap(axis, size, block, out, *take(3)))
+        else:
+            paired = kind == "paired"
+            rows = block.shape[0] // chunks
+            for chunk in range(chunks):
+                part = pl.ds(chunk * rows, rows)
+                flow = Line(
+                    axis, size, paired, block.at[part], ChunkedOut(out, part),
+                    *take(5 if paired else 3), *(() if paired else (None, None)),
+                )
+                flows.append(flow)
+        leaders.setdefault(axis, flows[-1])
+    barrier = pltpu.get_barrier_semaphore()
+    expected = 0
+    for flow in leaders.values():
+        expected = expected + flow.greet(barrier)
+    pl.semaphore_wait(barrier, expected)
+    run_flows(flows)
+
+
+class ChunkedOut:
+    def __init__(self, out, part):
+        self.out, self.part = out, part
+
+    @property
+    def at(self):
+        return self
+
+    def __getitem__(self, slot):
+        return self.out.at[slot, self.part]
+
+
 def move(identity, items):
     kinds, arrays, shapes, scratch = [], [], [], []
     sent = 0
-    for kind, axis, array in items:
+    for kind, axis, array, chunks in items:
         size = lax.axis_size(axis)
-        kinds.append((kind, axis, size))
+        kinds.append((kind, axis, size, chunks))
         arrays.append(array)
-        shape = array.shape if kind == "exchange" else (size,) + array.shape
-        shapes.append(jax.ShapeDtypeStruct(shape, array.dtype))
+        lead = {"exchange": (), "halo": (), "swap": (2,)}.get(kind, (size,))
+        shapes.append(jax.ShapeDtypeStruct(lead + array.shape, array.dtype))
         sent += array.size * array.dtype.itemsize
         dma = pltpu.SemaphoreType.DMA
         if kind == "exchange":
             scratch += [dma((size,)), dma((size,)), dma((1,))]
+        elif kind == "halo":
+            scratch += [dma((2,)), dma((2,))]
+        elif kind == "swap":
+            scratch += [dma((1,)), dma((1,)), dma((1,))]
         else:
-            length = size // 2 if kind == "paired" else size
-            steps = max(length - 1, 1)
-            scratch += [dma((2, steps)), dma((2, steps)), dma((1,))]
-            if kind == "paired":
-                scratch += [dma((2 * length,)), dma((2 * length,))]
+            scratch += line_scratch(size, kind == "paired") * chunks
     return pl.pallas_call(
         functools.partial(move_kernel, tuple(kinds)),
         out_shape=tuple(shapes),
@@ -285,6 +401,117 @@
         cost_estimate=pl.CostEstimate(flops=0, bytes_accessed=30 * sent, transcendentals=0),
         name=f"move{identity}",
     )(*arrays)
+
+
+def close_kernel(
+    axis, size, row_axis, row_size, chunks, part_ref, act_ref, project_ref, token_ref, rows_ref,
+    came_ref, sum_ref, total_ref, block_ref, send, recv, *line_sems,
+):
+    position = lax.axis_index(axis)
+    above, below = position > 0, position < size - 1
+    line = Line(row_axis, row_size, True, block_ref, rows_ref, *line_sems)
+    barrier = pltpu.get_barrier_semaphore()
+    expected = line.greet(barrier) + jnp.where(above, 1, 0) + jnp.where(below, 1, 0)
+    for present, target in ((above, position - 1), (below, position + 1)):
+
+        @pl.when(present)
+        def _():
+            pl.semaphore_signal(barrier, inc=1, device_id={axis: target}, device_id_type=MESH)
+
+    pl.semaphore_wait(barrier, expected)
+    height = part_ref.shape[1] // chunks
+    sides = ((above, 1), (below, -1))
+
+    def hop(side, step, chunk, relayed):
+        goal = size - 1 - step if side == 0 else step
+        rows = pl.ds(chunk * height, height)
+        source = sum_ref.at[side, goal, rows] if relayed else part_ref.at[goal, rows]
+        return pltpu.make_async_remote_copy(
+            src_ref=source,
+            dst_ref=came_ref.at[side, goal, rows],
+            send_sem=send.at[side, step, chunk],
+            recv_sem=recv.at[side, step, chunk],
+            device_id={axis: position + sides[side][1]},
+            device_id_type=MESH,
+        )
+
+    def each(action):
+        for step in range(size - 1):
+            goal_right, goal_left = size - 1 - step, step
+            for chunk in range(chunks):
+                for side in (0, 1):
+                    goal = goal_right if side == 0 else goal_left
+                    goes = position < goal if side == 0 else position > goal
+                    action(side, step, chunk, goal, goes, sides[side][0])
+
+    def forward(side, step, chunk, goal, goes, fed):
+        rows = pl.ds(chunk * height, height)
+
+        @pl.when(goes & fed)
+        def _():
+            hop(side, step, chunk, True).wait_recv()
+            sum_ref[side, goal, rows] = (
+                came_ref[side, goal, rows].astype(jnp.float32)
+                + part_ref[goal, rows].astype(jnp.float32)
+            ).astype(jnp.bfloat16)
+            hop(side, step, chunk, True).start()
+
+        @pl.when(goes & jnp.logical_not(fed))
+        def _():
+            hop(side, step, chunk, False).start()
+
+    each(forward)
+    total_ref[...] = act_ref[...].astype(jnp.float32) + part_ref[position].astype(jnp.float32)
+
+    def collect(side, step, chunk, goal, goes, fed):
+        rows = pl.ds(chunk * height, height)
+
+        @pl.when((position == goal) & fed)
+        def _():
+            hop(side, step, chunk, True).wait_recv()
+            total_ref[rows] = total_ref[rows] + came_ref[side, goal, rows].astype(jnp.float32)
+
+    each(collect)
+    token = total_ref[...].astype(jnp.bfloat16)
+    token_ref[...] = token
+    block_ref[...] = matmul(token, project_ref[...]).astype(jnp.bfloat16)
+    run_flows([line])
+
+    def settle(side, step, chunk, goal, goes, fed):
+        @pl.when(goes)
+        def _():
+            hop(side, step, chunk, True).wait_send()
+
+    each(settle)
+
+
+def close(identity, axis, row_axis, parts, act_rows, project):
+    size, row_size, chunks = lax.axis_size(axis), lax.axis_size(row_axis), 2
+    rows, depth = act_rows.shape
+    dma = pltpu.SemaphoreType.DMA
+    vmem = pl.BlockSpec(memory_space=pltpu.VMEM)
+    return pl.pallas_call(
+        functools.partial(close_kernel, axis, size, row_axis, row_size, chunks),
+        out_shape=(
+            jax.ShapeDtypeStruct((rows, depth), jnp.bfloat16),
+            jax.ShapeDtypeStruct((row_size, rows, project.shape[1]), jnp.bfloat16),
+        ),
+        in_specs=[vmem] * 3,
+        out_specs=(vmem, vmem),
+        scratch_shapes=[
+            pltpu.VMEM((2,) + parts.shape, jnp.bfloat16),
+            pltpu.VMEM((2,) + parts.shape, jnp.bfloat16),
+            pltpu.VMEM((rows, depth), jnp.float32),
+            pltpu.VMEM((rows, project.shape[1]), jnp.bfloat16),
+            dma((2, size - 1, chunks)),
+            dma((2, size - 1, chunks)),
+        ]
+        + line_scratch(row_size, True),
+        compiler_params=pltpu.CompilerParams(
+            collective_id=identity, has_side_effects=True, vmem_limit_bytes=VMEM_LIMIT
+        ),
+        name="close",
+    )(parts, act_rows, project)
 
 
 def attention_kernel(heads, span, q_ref, gate_ref, kv_ref, bias_ref, mask_ref, out_ref):
@@ -354,7 +581,7 @@
 
 
 def atom_kernel(
-    first_ref, bounds_ref, rows_ref, skip_ref, cond_ref, token_ref, weight_ref, vector_ref,
+    first_ref, bounds_ref, rows_ref, skip_ref, cond_ref, rim_ref, token_ref, weight_ref, vector_ref,
     position_ref, bias_ref, out_ref, state_ref, query_ref, gate_ref, key_ref, value_ref, held_ref,
 ):
     count, channels = query_ref.shape
@@ -368,9 +595,11 @@
         column = lax.broadcasted_iota(jnp.int32, (owners.shape[0], chunk), 1) + start
         hit = jnp.where(owners == column, 1.0, 0.0).astype(jnp.bfloat16)
         taken = taken + matmul(hit, rows_ref[start : start + chunk, :])
-    state = skip_ref[...].astype(jnp.float32) + taken
+    skip = jnp.concatenate([rim_ref[0, :, :channels], skip_ref[...], rim_ref[1, :, :channels]], axis=0)
+    cond = jnp.concatenate([rim_ref[0, :, channels:], cond_ref[...], rim_ref[1, :, channels:]], axis=0)
+    state = skip.astype(jnp.float32) + taken
     state_ref[...] = state
-    normed = layer_norm(cond_ref[...]).astype(jnp.bfloat16)
+    normed = layer_norm(cond).astype(jnp.bfloat16)
     atom_x = (
         jax.nn.sigmoid(matmul(normed, weight_ref[0]) + vector_ref[0:1, :]) * layer_norm(state)
         + matmul(normed, weight_ref[1])
@@ -384,34 +613,40 @@
     lane = lax.broadcasted_iota(jnp.int32, (1, WK), 1)
     scale = 1.0 / math.sqrt(head_width)
 
-    def window(index, carry):
-        base = pl.multiple_of(index * WQ, WQ)
-        queries = query_ref[pl.ds(base, WQ), :]
-        stacked = jnp.concatenate(
-            [jnp.where(head_of == head, queries, 0).astype(jnp.bfloat16) for head in range(HA)], axis=0
-        )
-        keys = key_ref[pl.ds(base, WK), :]
-        values = value_ref[pl.ds(base, WK), :]
-        scores = (
-            lax.dot_general(
-                stacked, keys, (((1,), (1,)), ((), ())), preferred_element_type=jnp.float32
+    def windows(step, carry):
+        scores = []
+        bases = [pl.multiple_of(step * (BATCH * WQ) + i * WQ, WQ) for i in range(BATCH)]
+        for i, base in enumerate(bases):
+            queries = query_ref[pl.ds(base, WQ), :]
+            stacked = jnp.concatenate(
+                [jnp.where(head_of == head, queries, 0).astype(jnp.bfloat16) for head in range(HA)],
+                axis=0,
             )
-            * scale
-        )
-        scores = scores + bias_ref[:, pl.ds(base, WQ), :].reshape(HA * WQ, WK).astype(jnp.float32)
-        slot = first_ref[0] + base - RIM + lane
-        inside = (slot >= bounds_ref[2 * index]) & (slot < bounds_ref[2 * index + 1])
-        scores = jnp.where(inside, scores, FAR)
-        weights = jnp.exp(scores - jnp.max(scores, axis=-1, keepdims=True))
-        totals = jnp.sum(weights, axis=-1, keepdims=True)
-        attended = matmul(weights.astype(jnp.bfloat16), values) / totals
-        result = jnp.zeros((WQ, channels), jnp.float32)
-        for head in range(HA):
-            result = result + jnp.where(head_of == head, attended[head * WQ : (head + 1) * WQ], 0.0)
-        held_ref[pl.ds(base, WQ), :] = result
+            score = lax.dot_general(
+                stacked, key_ref[pl.ds(base, WK), :], (((1,), (1,)), ((), ())),
+                preferred_element_type=jnp.float32,
+            )
+            bias = bias_ref[:, pl.ds(base, WQ), :].reshape(HA * WQ, WK).astype(jnp.float32)
+            slot = first_ref[0] + base - RIM + lane
+            index = step * BATCH + i
+            inside = (slot >= bounds_ref[2 * index]) & (slot < bounds_ref[2 * index + 1])
+            scores.append(jnp.where(inside, score * scale + bias, FAR))
+        weights = [jnp.exp(score - jnp.max(score, axis=-1, keepdims=True)) for score in scores]
+        results = []
+        for base, weight in zip(bases, weights):
+            attended = matmul(weight.astype(jnp.bfloat16), value_ref[pl.ds(base, WK), :])
+            attended = attended / jnp.sum(weight, axis=-1, keepdims=True)
+            result = jnp.zeros((WQ, channels), jnp.float32)
+            for head in range(HA):
+                result = result + jnp.where(
+                    head_of == head, attended[head * WQ : (head + 1) * WQ], 0.0
+                )
+            results.append(result)
+        start = pl.multiple_of(step * (BATCH * WQ), BATCH * WQ)
+        held_ref[pl.ds(start, BATCH * WQ), :] = jnp.concatenate(results, axis=0)
         return carry
 
-    lax.fori_loop(0, count // WQ, window, 0, unroll=UNROLL)
+    lax.fori_loop(0, count // (BATCH * WQ), windows, 0)
     gated = (held_ref[...] * jax.nn.sigmoid(gate_ref[...].astype(jnp.float32))).astype(jnp.bfloat16)
     fresh = state_ref[inner, :] + matmul(gated, weight_ref[6])
     final = layer_norm(fresh).astype(jnp.bfloat16)
@@ -420,17 +655,17 @@
     )
 
 
-UNROLL = 8
-
-
-def atom_block(first, bounds, rows, skip, cond, owners, weights, vectors, positions, bias):
+BATCH = 8
+
+
+def atom_block(first, bounds, rows, skip, cond, rims, owners, weights, vectors, positions, bias):
     count, channels = bias.shape[1], skip.shape[1]
-    extended = skip.shape[0]
+    extended = skip.shape[0] + 2 * RIM
     smem = pl.BlockSpec(memory_space=pltpu.SMEM)
     vmem = pl.BlockSpec(memory_space=pltpu.VMEM)
     return pl.pallas_call(
         atom_kernel,
-        in_specs=[smem, smem] + [vmem] * 8,
+        in_specs=[smem, smem] + [vmem] * 9,
         out_specs=vmem,
         out_shape=jax.ShapeDtypeStruct((positions.shape[0], count), jnp.float32),
         scratch_shapes=[
@@ -443,16 +678,11 @@
         ],
         compiler_params=pltpu.CompilerParams(vmem_limit_bytes=VMEM_LIMIT),
         name="atom_block",
-    )(first, bounds, rows, skip, cond, owners, weights, vectors, positions, bias)
-
-
-def rim_extended(array, axis):
-    size, length = (lax.axis_size(axis), array.shape[0])
-    up = [(i, (i + 1) % size) for i in range(size - 1)]
-    down = [(j, i) for i, j in up]
-    before = lax.ppermute(array[length - RIM :], axis, up)
-    after = lax.ppermute(array[:RIM], axis, down)
-    return jnp.concatenate([before, array, after], axis=0)
+    )(first, bounds, rows, skip, cond, rims, owners, weights, vectors, positions, bias)
+
+
+def rims(array):
+    return jnp.stack([array[:RIM], array[array.shape[0] - RIM :]])
 
 
 def per_device(
@@ -482,20 +712,27 @@
     column_count = attention_in.shape[2]
     channels = atom_cond.shape[1]
     start = lax.axis_index("fsdp") * column_count
-    atom_pair = rim_extended(jnp.concatenate([atom_skip[0], atom_cond], axis=1), "seq")
-    owners = rim_extended(atom_token, "seq")[:, None]
+    atom_rims = rims(jnp.concatenate([atom_skip[0], atom_cond], axis=1))
+    owner_rims = jnp.pad(rims(atom_token)[:, None, :], ((0, 0), (0, 0), (0, 2 * WK - RIM)))
+    small = jnp.concatenate([atom_weights.reshape(-1, channels), token_to_atom], axis=0)
+    small_height = small.shape[0] // 2
+    small_half = lax.dynamic_slice_in_dim(
+        small, lax.rem(lax.axis_index("seq"), 2) * small_height, small_height
+    )
 
     cond_normed = layer_norm(token_cond[0]).astype(jnp.bfloat16)
     act_normed = layer_norm(act_rows).astype(jnp.bfloat16)
     act_slots = jnp.transpose(act_normed.reshape(row_count, groups, column_count), (1, 0, 2))
-    cond_all, act_all, mask_all = move(
+    cond_all, act_all, atom_rims, owner_rims = move(
         1,
         (
-            ("line", "fsdp", cond_normed),
-            ("exchange", "fsdp", pack(act_slots)),
-            ("paired", "seq", token_mask[None]),
+            ("line", "fsdp", cond_normed, 4),
+            ("exchange", "fsdp", pack(act_slots), 1),
+            ("halo", "seq", atom_rims, 1),
+            ("halo", "seq", owner_rims, 1),
         ),
     )
+    owners = jnp.concatenate([owner_rims[0, 0, :RIM], atom_token, owner_rims[1, 0, :RIM]])[:, None]
     cond_flat = cond_all.reshape(groups * row_count, depth)
     act_flat = unpack(act_all).reshape(groups * row_count, column_count).astype(jnp.float32)
 
@@ -509,7 +746,9 @@
         array = unpack(array)
         return jnp.transpose(array, (1, 2, 0, 3)).reshape(groups * row_count, depth)
 
-    (attend_all,) = move(2, (("line", "fsdp", adaptive(0, 1, 0)),))
+    attend_all, small_halves = move(
+        2, (("line", "fsdp", adaptive(0, 1, 0), groups), ("line", "fsdp", small_half, 1))
+    )
     transit_part = adaptive(2, 3, 1)
     attend_flat = joined(attend_all)
     query_bias = lax.dynamic_slice_in_dim(token_vectors[2], start, column_count)
@@ -521,24 +760,16 @@
         return array.astype(jnp.bfloat16).reshape(groups, row_count, -1)
 
     keys_values = jnp.concatenate([grouped(project(1)), grouped(project(2))], axis=-1)
-    kv_all, transit_all, small_all = move(
+    kv_all, transit_all, mask_all, small_all = move(
         3,
         (
-            ("paired", "seq", keys_values),
-            ("line", "fsdp", transit_part),
-            (
-                "line",
-                "fsdp",
-                jnp.concatenate(
-                    [
-                        atom_weights.reshape(-1, channels),
-                        token_to_atom,
-                    ],
-                    axis=0,
-                ),
-            ),
+            ("paired", "seq", keys_values, groups),
+            ("line", "fsdp", transit_part, groups),
+            ("paired", "seq", token_mask[None], 1),
+            ("swap", "seq", small_halves, 1),
         ),
     )
+    small_all = jnp.transpose(small_all, (1, 0, 2, 3)).reshape(groups, -1, channels)
     query_rows = grouped(project(0) + query_bias)
     gate_rows = grouped(project(3))
     weight_rows = atom_weights.size // channels
@@ -554,21 +785,22 @@
         jax.nn.silu(matmul(transit_flat, transition_in[0])) * matmul(transit_flat, transition_in[1])
     ).astype(jnp.bfloat16)
     partial_sum = matmul(gated, attention_out) + matmul(hidden, transition_out)
-    (parts,) = move(
+    token_result, all_rows = close(
         4,
-        (("exchange", "fsdp", partial_sum.astype(jnp.bfloat16).reshape(groups, row_count, depth)),),
-    )
-    combined = jnp.sum(parts.astype(jnp.float32), axis=0)
-    token_result = (act_rows.astype(jnp.float32) + combined).astype(jnp.bfloat16)
-    projected = matmul(token_result, project_full).astype(jnp.bfloat16)
-    (all_rows,) = move(5, (("paired", "seq", projected),))
+        "fsdp",
+        "seq",
+        partial_sum.astype(jnp.bfloat16).reshape(groups, row_count, depth),
+        act_rows,
+        project_full,
+    )
     first_atom = (lax.axis_index("seq") * atom_cond.shape[0]).astype(jnp.int32).reshape(1)
     update = atom_block(
         first_atom,
         window_bounds.reshape(-1),
         all_rows.reshape(-1, channels),
-        atom_pair[:, :channels],
-        atom_pair[:, channels:],
+        atom_skip[0],
+        atom_cond,
+        atom_rims,
         owners,
         atom_full,
         atom_vectors,

time: 171 us -> 153 us (0.89)
  starting transfers between devices: 10.7 us -> 0 us
  Pallas kernels: 117 us -> 110 us
    pallas_call x5 -> x3, Pallas kernels: 98.5 us -> 66.9 us  [move(): pl.pallas_call(functools.partial(move_kernel, tuple(kinds)), out_shape=tu...]
    pallas_call x1 -> x2, Pallas kernels: 12.4 us -> 37.1 us  [the longest x1 30.5 us: close(): pl.pallas_call(functools.partial(close_kernel, axis, size, row_axis, row_...]
    ppermute x4 -> x0, starting transfers between devices: 10.7 us -> none  [the longest x2 6.91 us: rim_extended(): before = lax.ppermute(array[length - RIM:], axis, up)]
    unnamed x39 -> x45, local copies, waits for them, and re-layouts: 2.43 us -> 4.69 us
    dot_general x12 -> x11, matrix products: 15 us -> 14.7 us  [matmul(): return jnp.dot(left_side, right_side, preferred_element_type=jnp.float32)]
  transfers between devices with their start and end apart: 4 -> 0, of which waited for: 0 -> 0; matrix products, arithmetic and copies ran while one was open for 21% -> 0% of each run, Pallas kernels for 62% -> 0%
where the time goes in v2:
time: 153 us; the launch traced here: 152 us
  Pallas kernels  110 us (72%)
  local copies, waits for them, and re-layouts  17.1 us (11%)
  matrix products  14.7 us (10%)
  other arithmetic  9.65 us (6%)
    pallas_call x3, Pallas kernels, move(): pl.pallas_call(functools.partial(move_kernel, tuple(kinds)), out_shape=tu...  66.9 us
    pallas_call x1, Pallas kernels, close(): pl.pallas_call(functools.partial(close_kernel, axis, size, row_axis, row_...  30.5 us
    dot_general x11, matrix products, matmul(): return jnp.dot(left_side, right_side, preferred_element_type=jnp.float32)  14.7 us
    pallas_call x1, Pallas kernels, atom_block(): pl.pallas_call(atom_kernel, in_specs=[smem, smem] + [vmem] * 9, out_specs...  6.57 us
    pallas_call x1, Pallas kernels, token_attention(): pl.pallas_call(functools.partial(attention_kernel, heads, max(512 // piec...  5.7 us
    unnamed x45, local copies, waits for them, and re-layouts  4.69 us

profile of v2, /device:TPU:1, one launch (start us, length us, event | category | flops | bytes accessed | tf_op | source)
XLA Modules:
  0.0 152.3 jit_solution(9360934533108627688)
XLA Ops:
  0.7 1.1 convert_reduce_fusion.1
  1.8 1.1 fusion.43
  2.9 1.8 %fusion.44.refs_0_ = bf16[128,768]{1,0:T(8,128)(2,1)} fusion(bf16[1,128,768]{2,1,0:T(8,128)(2,1)} %param.20, f32[128]{0:T(128)S(1)} %add_rsqrt_fusion.1, f32[128]{0:T(128)S(1)} %broadcast_multiply_fusion.1), kind=kLoop, calls=%fused_computation.57 | loop fusion | flops 393216 | bytes 394240 | tf_op jit(solution)/shard_map/convert_element_type | solution.py:723
  4.7 1.1 copy.53
  8.6 23.5 %move1.1 = (bf16[4,128,768]{2,1,0:T(8,128)(2,1)}, bf16[4,64,384]{2,1,0:T(8,128)(2,1)}, bf16[2,48,256]{2,1,0:T(8,128)(2,1)}, s32[2,1,256]{2,1,0:T(1,128)}) custom-call(bf16[128,768]{1,0:T(8,128)(2,1)} %fusion.44.refs_0_, bf16[4,64,384]{2,1,0:T(8,128)(2,1)} %pad_maximum_fusion.2.refs_1_, bf16[2,48,256]{2,1,0:T(8,128)(2,1)} %pad_maximum_fusion.5.refs_2_, ...), custom_call_target="tpu_custom_call" | custom-call | bytes 13332480 | tf_op jit(solution)/shard_map/move1/pallas_call | solution.py:392
  32.0 1.1 fusion.73
  37.9 19.7 %move2.1 = (bf16[4,4,64,384]{3,2,1,0:T(8,128)(2,1)}, bf16[4,208,128]{2,1,0:T(8,128)(2,1)}) custom-call(bf16[4,64,384]{2,1,0:T(8,128)(2,1)} %pad_maximum_fusion.3.refs_0_, bf16[208,128]{1,0:T(8,128)(2,1)} %fusion.65.refs_1_), custom_call_target="tpu_custom_call" | custom-call | bytes 7495680 | tf_op jit(solution)/shard_map/move2/pallas_call | solution.py:392
  57.6 1.5 fusion.69
  60.0 1.4 fusion.13
  63.9 1.3 convolution_convert_fusion.1
  65.3 0.9 pad_maximum_fusion.refs_0_
  66.3 1.4 fusion.5
  67.7 1.4 fusion.12
  70.0 23.8 %move3.1 = (bf16[4,4,128,384]{3,2,1,0:T(8,128)(2,1)}, bf16[4,4,64,384]{3,2,1,0:T(8,128)(2,1)}, s32[4,1,128]{2,1,0:T(1,128)}, bf16[2,4,208,128]{3,2,1,0:T(8,128)(2,1)}) custom-call(bf16[4,128,384]{2,1,0:T(8,128)(2,1)} %pad_maximum_fusion.refs_0_, bf16[4,64,384]{2,1,0:T(8,128)(2,1)} %pad_maximum_fusion.4.refs_1_, s32[1,128]{1,0:T(1,128)} %bitcast.162, ...), custom_call_target="tpu_custom_call" | custom-call | bytes 24099840 | tf_op jit(solution)/shard_map/move3/pallas_call | solution.py:392
  93.8 5.7 %token_attention.1 = bf16[4,128,192]{2,1,0:T(8,128)(2,1)} custom-call(bf16[4,128,192]{2,1,0:T(8,128)(2,1)} %bitcast.134, bf16[4,128,192]{2,1,0:T(8,128)(2,1)} %bitcast.135, bf16[4,4,128,384]{3,2,1,0:T(8,128)(2,1)} %get-tuple-element.18.kv_ref, bf16[4,128,512]{2,1,0:T(8,128)(2,1)} %bias_ref.2, s32[1,512]{1,0:T(1,128)} %bitcast.158), custom_call_target="tpu_custom_call" | custom-call | tf_op jit(solution)/shard_map/token_attention/pallas_call | solution.py:566
  99.5 1.4 fusion.75
  101.4 1.3 copy.67
  102.7 2.9 %fusion.16 = f32[512,384]{1,0:T(8,128)} fusion(bf16[96,8,4,128]{3,2,1,0:T(4,128)(2,1)} %bitcast.148, bf16[2,768,384]{2,1,0:T(8,128)(2,1)} %param.26), kind=kOutput, calls=%fused_computation.27 | convolution fusion | flops 301989888 | bytes 2162688 | tf_op jit(solution)/shard_map/dot_general | solution.py:30
  105.6 3.4 %add_convert_fusion = bf16[512,768]{1,0:T(8,128)(2,1)} fusion(f32[512,768]{1,0:T(8,128)S(1)} %fusion.75, bf16[384,768]{1,0:T(8,128)(2,1)S(1)} %copy-done, f32[512,384]{1,0:T(8,128)} %fusion.16, bf16[96,8,4,128]{3,2,1,0:T(4,128)(2,1)S(1)} %bitcast.149, bf16[2,768,384]{2,1,0:T(8,128)(2,1)} %param.26), kind=kOutput, calls=%fused_computation | convolution fusion | flops 605945856 | bytes 5111808 | tf_op jit(solution)/shard_map/dot_general | solution.py:30
  109.7 30.5 %close.1 = (bf16[128,768]{1,0:T(8,128)(2,1)}, bf16[4,128,128]{2,1,0:T(8,128)(2,1)}) custom-call(bf16[4,128,768]{2,1,0:T(8,128)(2,1)} %bitcast.151, bf16[128,768]{1,0:T(8,128)(2,1)} %bitcast.131, bf16[768,128]{1,0:T(8,128)(2,1)} %bitcast.150), custom_call_target="tpu_custom_call" | custom-call | tf_op jit(solution)/shard_map/close/pallas_call | solution.py:493
  141.1 1.0 broadcast_in_dim.27.token_ref
  142.8 0.8 copy.72.weight_ref
  143.7 6.6 %atom_block.1 = f32[3,1024]{1,0:T(4,128)} custom-call(s32[1]{0:T(128)} %bitcast.43.first_ref, s32[64]{0:T(128)} %reshape.128.bounds_ref, bf16[512,128]{1,0:T(8,128)(2,1)} %bitcast.155, bf16[1024,128]{1,0:T(8,128)(2,1)} %bitcast.141, bf16[1024,128]{1,0:T(8,128)(2,1)} %cond_ref.1, bf16[2,48,256]{2,1,0:T(8,128)(2,1)} %get-tuple-element.24.rim_ref, ...), custom_call_target="tpu_custom_call" | custom-call | tf_op jit(solution)/shard_map/atom_block/pallas_call | solution.py:666
  150.3 1.3 copy.73
  (92 shorter events, 15.2 us)
Async XLA Ops:
  0.6 105.0 %copy-start = (bf16[384,768]{1,0:T(8,128)(2,1)S(1)}, bf16[384,768]{1,0:T(8,128)(2,1)}, u32[]{:S(2)}) copy-start(bf16[384,768]{1,0:T(8,128)(2,1)} %param.27) | copy-start | bytes 1769476
  0.6 5.3 %copy-start.2 = (bf16[1,128,768]{2,1,0:T(8,128)(2,1)S(1)}, bf16[1,128,768]{2,1,0:T(8,128)(2,1)}, u32[]{:S(2)}) copy-start(bf16[1,128,768]{2,1,0:T(8,128)(2,1)} %param.19) | copy-start | bytes 589828
  5.9 1.3 copy-start.4
  6.0 1.3 copy-start.5
  6.3 1.6 %copy-start.16 = (s32[1024]{0:T(1024)S(1)}, s32[1024]{0:T(1024)}, u32[]{:S(2)}) copy-start(s32[1024]{0:T(1024)} %param.33) | copy-start | bytes 12292
  33.1 0.7 copy-start.15
  33.1 1.1 copy-start.1
  33.1 1.7 %copy-start.10 = (bf16[4,768,192]{1,2,0:T(8,128)(2,1)S(1)}, bf16[4,768,192]{1,2,0:T(8,128)(2,1)}, u32[]{:S(2)}) copy-start(bf16[4,768,192]{1,2,0:T(8,128)(2,1)} %param.23) | copy-start | bytes 3538948
  33.5 1.8 %copy-start.8 = (f32[512,192]{0,1:T(8,128)}, f32[512,192]{0,1:T(8,128)S(1)}, u32[]{:S(2)}) copy-start(f32[512,192]{0,1:T(8,128)S(1)} %copy.57) | copy-start | bytes 1179652
  35.3 1.4 copy-start.13
  35.7 1.3 copy-start.14
  59.9 2.3 %copy-start.19 = (bf16[4,768,192]{1,2,0:T(8,128)(2,1)S(1)}, bf16[4,768,192]{1,2,0:T(8,128)(2,1)}, u32[]{:S(2)}) copy-start(bf16[4,768,192]{1,2,0:T(8,128)(2,1)} %param.24) | copy-start | bytes 3538948
  63.8 2.4 %copy-start.9 = (f32[512,192]{0,1:T(8,128)S(1)}, f32[512,192]{0,1:T(8,128)}, u32[]{:S(2)}) copy-start(f32[512,192]{0,1:T(8,128)} %copy-done.8) | copy-start | bytes 1179652
  93.8 5.7 %copy-start.11 = (bf16[192,768]{1,0:T(8,128)(2,1)S(1)}, bf16[192,768]{1,0:T(8,128)(2,1)}, u32[]{:S(2)}) copy-start(bf16[192,768]{1,0:T(8,128)(2,1)} %param.25) | copy-start | bytes 884740
  99.5 1.4 copy-start.3
  102.7 2.9 %copy-start.6 = (bf16[4,128,4,192]{1,0,3,2:T(4,128)(2,1)S(1)}, bf16[4,128,4,192]{1,0,3,2:T(4,128)(2,1)}, u32[]{:S(2)}) copy-start(bf16[4,128,4,192]{1,0,3,2:T(4,128)(2,1)} %copy.67) | copy-start | bytes 2359300
  105.6 3.4 %copy-start.7 = (bf16[2,4,208,128]{3,2,1,0:T(8,128)(2,1)S(1)}, bf16[2,4,208,128]{3,2,1,0:T(8,128)(2,1)}, u32[]{:S(2)}) copy-start(bf16[2,4,208,128]{3,2,1,0:T(8,128)(2,1)} %get-tuple-element.21) | copy-start | bytes 1277956
  109.0 31.2 %copy-start.17 = (s32[32,2]{0,1:T(2,128)S(1)}, s32[32,2]{0,1:T(2,128)}, u32[]{:S(2)}) copy-start(s32[32,2]{0,1:T(2,128)} %param.32) | copy-start | bytes 772
  109.0 32.0 %copy-start.18 = (s32[2,1,256]{2,1,0:T(1,128)S(1)}, s32[2,1,256]{2,1,0:T(1,128)}, u32[]{:S(2)}) copy-start(s32[2,1,256]{2,1,0:T(1,128)} %get-tuple-element.25) | copy-start | bytes 6148
  143.7 7.9 %copy-start.12 = (bf16[128,768]{1,0:T(8,128)(2,1)S(1)}, bf16[128,768]{1,0:T(8,128)(2,1)}, u32[]{:S(2)}) copy-start(bf16[128,768]{1,0:T(8,128)(2,1)} %get-tuple-element.22) | copy-start | bytes 589828

commit v3 on v2

--- a/solution.py
+++ b/solution.py
@@ -404,94 +404,32 @@
 
 
 def close_kernel(
-    axis, size, row_axis, row_size, chunks, part_ref, act_ref, project_ref, token_ref, rows_ref,
-    came_ref, sum_ref, total_ref, block_ref, send, recv, *line_sems,
+    axis, size, row_axis, row_size, part_ref, act_ref, project_ref, token_ref, rows_ref,
+    came_ref, block_ref, send, recv, local, *line_sems,
 ):
-    position = lax.axis_index(axis)
-    above, below = position > 0, position < size - 1
     line = Line(row_axis, row_size, True, block_ref, rows_ref, *line_sems)
+    swap = Exchange(axis, size, part_ref, came_ref, send, recv, local)
     barrier = pltpu.get_barrier_semaphore()
-    expected = line.greet(barrier) + jnp.where(above, 1, 0) + jnp.where(below, 1, 0)
-    for present, target in ((above, position - 1), (below, position + 1)):
-
-        @pl.when(present)
-        def _():
-            pl.semaphore_signal(barrier, inc=1, device_id={axis: target}, device_id_type=MESH)
-
+    expected = line.greet(barrier) + swap.greet(barrier)
     pl.semaphore_wait(barrier, expected)
-    height = part_ref.shape[1] // chunks
-    sides = ((above, 1), (below, -1))
-
-    def hop(side, step, chunk, relayed):
-        goal = size - 1 - step if side == 0 else step
-        rows = pl.ds(chunk * height, height)
-        source = sum_ref.at[side, goal, rows] if relayed else part_ref.at[goal, rows]
-        return pltpu.make_async_remote_copy(
-            src_ref=source,
-            dst_ref=came_ref.at[side, goal, rows],
-            send_sem=send.at[side, step, chunk],
-            recv_sem=recv.at[side, step, chunk],
-            device_id={axis: position + sides[side][1]},
-            device_id_type=MESH,
-        )
-
-    def each(action):
-        for step in range(size - 1):
-            goal_right, goal_left = size - 1 - step, step
-            for chunk in range(chunks):
-                for side in (0, 1):
-                    goal = goal_right if side == 0 else goal_left
-                    goes = position < goal if side == 0 else position > goal
-                    action(side, step, chunk, goal, goes, sides[side][0])
-
-    def forward(side, step, chunk, goal, goes, fed):
-        rows = pl.ds(chunk * height, height)
-
-        @pl.when(goes & fed)
-        def _():
-            hop(side, step, chunk, True).wait_recv()
-            sum_ref[side, goal, rows] = (
-                came_ref[side, goal, rows].astype(jnp.float32)
-                + part_ref[goal, rows].astype(jnp.float32)
-            ).astype(jnp.bfloat16)
-            hop(side, step, chunk, True).start()
-
-        @pl.when(goes & jnp.logical_not(fed))
-        def _():
-            hop(side, step, chunk, False).start()
-
-    each(forward)
-    total_ref[...] = act_ref[...].astype(jnp.float32) + part_ref[position].astype(jnp.float32)
-
-    def collect(side, step, chunk, goal, goes, fed):
-        rows = pl.ds(chunk * height, height)
-
-        @pl.when((position == goal) & fed)
-        def _():
-            hop(side, step, chunk, True).wait_recv()
-            total_ref[rows] = total_ref[rows] + came_ref[side, goal, rows].astype(jnp.float32)
-
-    each(collect)
-    token = total_ref[...].astype(jnp.bfloat16)
+    swap.begin()
+    swap.finish()
+    total = act_ref[...].astype(jnp.float32)
+    for origin in range(size):
+        total = total + came_ref[origin].astype(jnp.float32)
+    token = total.astype(jnp.bfloat16)
     token_ref[...] = token
     block_ref[...] = matmul(token, project_ref[...]).astype(jnp.bfloat16)
     run_flows([line])
 
-    def settle(side, step, chunk, goal, goes, fed):
-        @pl.when(goes)
-        def _():
-            hop(side, step, chunk, True).wait_send()
-
-    each(settle)
-
 
 def close(identity, axis, row_axis, parts, act_rows, project):
-    size, row_size, chunks = lax.axis_size(axis), lax.axis_size(row_axis), 2
+    size, row_size = lax.axis_size(axis), lax.axis_size(row_axis)
     rows, depth = act_rows.shape
     dma = pltpu.SemaphoreType.DMA
     vmem = pl.BlockSpec(memory_space=pltpu.VMEM)
     return pl.pallas_call(
-        functools.partial(close_kernel, axis, size, row_axis, row_size, chunks),
+        functools.partial(close_kernel, axis, size, row_axis, row_size),
         out_shape=(
             jax.ShapeDtypeStruct((rows, depth), jnp.bfloat16),
             jax.ShapeDtypeStruct((row_size, rows, project.shape[1]), jnp.bfloat16),
@@ -499,12 +437,11 @@
         in_specs=[vmem] * 3,
         out_specs=(vmem, vmem),
         scratch_shapes=[
-            pltpu.VMEM((2,) + parts.shape, jnp.bfloat16),
-            pltpu.VMEM((2,) + parts.shape, jnp.bfloat16),
-            pltpu.VMEM((rows, depth), jnp.float32),
+            pltpu.VMEM(parts.shape, jnp.bfloat16),
             pltpu.VMEM((rows, project.shape[1]), jnp.bfloat16),
-            dma((2, size - 1, chunks)),
-            dma((2, size - 1, chunks)),
+            dma((size,)),
+            dma((size,)),
+            dma((1,)),
         ]
         + line_scratch(row_size, True),
         compiler_params=pltpu.CompilerParams(

time: 153 us -> 148 us (0.967); the launches traced: 152 us -> 145 us
  Pallas kernels: 110 us -> 102 us
    pallas_call x1, Pallas kernels: 30.5 us -> 23.3 us  [close(): pl.pallas_call(functools.partial(close_kernel, axis, size, row_axis, row_...]
where the time goes in v3:
time: 148 us; the launch traced here: 145 us
  Pallas kernels  102 us (69%)
  local copies, waits for them, and re-layouts  17.1 us (12%)
  matrix products  14.7 us (10%)
  other arithmetic  9.65 us (7%)
    pallas_call x3, Pallas kernels, move(): pl.pallas_call(functools.partial(move_kernel, tuple(kinds)), out_shape=tu...  66.9 us
    pallas_call x1, Pallas kernels, close(): pl.pallas_call(functools.partial(close_kernel, axis, size, row_axis, row_...  23.3 us
    dot_general x11, matrix products, matmul(): return jnp.dot(left_side, right_side, preferred_element_type=jnp.float32)  14.7 us
    pallas_call x1, Pallas kernels, atom_block(): pl.pallas_call(atom_kernel, in_specs=[smem, smem] + [vmem] * 9, out_specs...  6.57 us
    pallas_call x1, Pallas kernels, token_attention(): pl.pallas_call(functools.partial(attention_kernel, heads, max(512 // piec...  5.7 us
    unnamed x45, local copies, waits for them, and re-layouts  4.69 us

profile of v3, /device:TPU:1, one launch (start us, length us, event | category | flops | bytes accessed | tf_op | source)
XLA Modules:
  0.0 145.0 jit_solution(5804265202366672812)
XLA Ops:
  0.7 1.1 convert_reduce_fusion.1
  1.8 1.1 fusion.43
  2.9 1.8 %fusion.44.refs_0_ = bf16[128,768]{1,0:T(8,128)(2,1)} fusion(bf16[1,128,768]{2,1,0:T(8,128)(2,1)} %param.20, f32[128]{0:T(128)S(1)} %add_rsqrt_fusion.1, f32[128]{0:T(128)S(1)} %broadcast_multiply_fusion.1), kind=kLoop, calls=%fused_computation.57 | loop fusion | flops 393216 | bytes 394240 | tf_op jit(solution)/shard_map/convert_element_type | solution.py:660
  4.7 1.1 copy.53
  8.6 23.5 %move1.1 = (bf16[4,128,768]{2,1,0:T(8,128)(2,1)}, bf16[4,64,384]{2,1,0:T(8,128)(2,1)}, bf16[2,48,256]{2,1,0:T(8,128)(2,1)}, s32[2,1,256]{2,1,0:T(1,128)}) custom-call(bf16[128,768]{1,0:T(8,128)(2,1)} %fusion.44.refs_0_, bf16[4,64,384]{2,1,0:T(8,128)(2,1)} %pad_maximum_fusion.2.refs_1_, bf16[2,48,256]{2,1,0:T(8,128)(2,1)} %pad_maximum_fusion.5.refs_2_, ...), custom_call_target="tpu_custom_call" | custom-call | bytes 13332480 | tf_op jit(solution)/shard_map/move1/pallas_call | solution.py:392
  32.0 1.1 fusion.73
  37.9 19.7 %move2.1 = (bf16[4,4,64,384]{3,2,1,0:T(8,128)(2,1)}, bf16[4,208,128]{2,1,0:T(8,128)(2,1)}) custom-call(bf16[4,64,384]{2,1,0:T(8,128)(2,1)} %pad_maximum_fusion.3.refs_0_, bf16[208,128]{1,0:T(8,128)(2,1)} %fusion.65.refs_1_), custom_call_target="tpu_custom_call" | custom-call | bytes 7495680 | tf_op jit(solution)/shard_map/move2/pallas_call | solution.py:392
  57.6 1.5 %fusion.69 = (bf16[4,4,64,192]{3,2,1,0:T(8,128)(2,1)S(1)}, bf16[4,4,64,192]{3,2,1,0:T(8,128)(2,1)S(1)}) fusion(bf16[4,4,64,384]{3,2,1,0:T(8,128)(2,1)} %get-tuple-element.16), kind=kLoop, calls=%fused_computation.105 | loop fusion | bytes 1572864 | tf_op jit(solution)/shard_map/slice | solution.py:40
  60.0 1.4 fusion.13
  63.9 1.3 convolution_convert_fusion.1
  65.3 0.9 pad_maximum_fusion.refs_0_
  66.3 1.4 fusion.5
  67.7 1.4 fusion.12
  70.0 23.8 %move3.1 = (bf16[4,4,128,384]{3,2,1,0:T(8,128)(2,1)}, bf16[4,4,64,384]{3,2,1,0:T(8,128)(2,1)}, s32[4,1,128]{2,1,0:T(1,128)}, bf16[2,4,208,128]{3,2,1,0:T(8,128)(2,1)}) custom-call(bf16[4,128,384]{2,1,0:T(8,128)(2,1)} %pad_maximum_fusion.refs_0_, bf16[4,64,384]{2,1,0:T(8,128)(2,1)} %pad_maximum_fusion.4.refs_1_, s32[1,128]{1,0:T(1,128)} %bitcast.162, ...), custom_call_target="tpu_custom_call" | custom-call | bytes 24099840 | tf_op jit(solution)/shard_map/move3/pallas_call | solution.py:392
  93.8 5.7 %token_attention.1 = bf16[4,128,192]{2,1,0:T(8,128)(2,1)} custom-call(bf16[4,128,192]{2,1,0:T(8,128)(2,1)} %bitcast.134, bf16[4,128,192]{2,1,0:T(8,128)(2,1)} %bitcast.135, bf16[4,4,128,384]{3,2,1,0:T(8,128)(2,1)} %get-tuple-element.18.kv_ref, bf16[4,128,512]{2,1,0:T(8,128)(2,1)} %bias_ref.2, s32[1,512]{1,0:T(1,128)} %bitcast.158), custom_call_target="tpu_custom_call" | custom-call | tf_op jit(solution)/shard_map/token_attention/pallas_call | solution.py:503
  99.5 1.4 fusion.75
  101.4 1.3 copy.67
  102.7 2.9 %fusion.16 = f32[512,384]{1,0:T(8,128)} fusion(bf16[96,8,4,128]{3,2,1,0:T(4,128)(2,1)} %bitcast.148, bf16[2,768,384]{2,1,0:T(8,128)(2,1)} %param.26), kind=kOutput, calls=%fused_computation.27 | convolution fusion | flops 301989888 | bytes 2162688 | tf_op jit(solution)/shard_map/dot_general | solution.py:30
  105.6 3.4 %add_convert_fusion = bf16[512,768]{1,0:T(8,128)(2,1)} fusion(f32[512,768]{1,0:T(8,128)S(1)} %fusion.75, bf16[384,768]{1,0:T(8,128)(2,1)S(1)} %copy-done, f32[512,384]{1,0:T(8,128)} %fusion.16, bf16[96,8,4,128]{3,2,1,0:T(4,128)(2,1)S(1)} %bitcast.149, bf16[2,768,384]{2,1,0:T(8,128)(2,1)} %param.26), kind=kOutput, calls=%fused_computation | convolution fusion | flops 605945856 | bytes 5111808 | tf_op jit(solution)/shard_map/dot_general | solution.py:30
  109.7 23.3 %close.1 = (bf16[128,768]{1,0:T(8,128)(2,1)}, bf16[4,128,128]{2,1,0:T(8,128)(2,1)}) custom-call(bf16[4,128,768]{2,1,0:T(8,128)(2,1)} %bitcast.151, bf16[128,768]{1,0:T(8,128)(2,1)} %bitcast.131, bf16[768,128]{1,0:T(8,128)(2,1)} %bitcast.150), custom_call_target="tpu_custom_call" | custom-call | tf_op jit(solution)/shard_map/close/pallas_call | solution.py:431
  133.8 1.0 broadcast_in_dim.27.token_ref
  135.6 0.8 copy.72.weight_ref
  136.4 6.6 %atom_block.1 = f32[3,1024]{1,0:T(4,128)} custom-call(s32[1]{0:T(128)} %bitcast.43.first_ref, s32[64]{0:T(128)} %reshape.128.bounds_ref, bf16[512,128]{1,0:T(8,128)(2,1)} %bitcast.155, bf16[1024,128]{1,0:T(8,128)(2,1)} %bitcast.141, bf16[1024,128]{1,0:T(8,128)(2,1)} %cond_ref.1, bf16[2,48,256]{2,1,0:T(8,128)(2,1)} %get-tuple-element.24.rim_ref, ...), custom_call_target="tpu_custom_call" | custom-call | tf_op jit(solution)/shard_map/atom_block/pallas_call | solution.py:603
  143.0 1.3 copy.73
  (92 shorter events, 15.2 us)
Async XLA Ops:
  0.6 105.0 %copy-start = (bf16[384,768]{1,0:T(8,128)(2,1)S(1)}, bf16[384,768]{1,0:T(8,128)(2,1)}, u32[]{:S(2)}) copy-start(bf16[384,768]{1,0:T(8,128)(2,1)} %param.27) | copy-start | bytes 1769476
  0.6 5.3 %copy-start.2 = (bf16[1,128,768]{2,1,0:T(8,128)(2,1)S(1)}, bf16[1,128,768]{2,1,0:T(8,128)(2,1)}, u32[]{:S(2)}) copy-start(bf16[1,128,768]{2,1,0:T(8,128)(2,1)} %param.19) | copy-start | bytes 589828
  5.9 1.3 copy-start.4
  6.0 1.3 copy-start.5
  6.3 1.6 %copy-start.16 = (s32[1024]{0:T(1024)S(1)}, s32[1024]{0:T(1024)}, u32[]{:S(2)}) copy-start(s32[1024]{0:T(1024)} %param.33) | copy-start | bytes 12292
  33.1 0.7 copy-start.15
  33.1 1.1 copy-start.1
  33.1 1.7 %copy-start.10 = (bf16[4,768,192]{1,2,0:T(8,128)(2,1)S(1)}, bf16[4,768,192]{1,2,0:T(8,128)(2,1)}, u32[]{:S(2)}) copy-start(bf16[4,768,192]{1,2,0:T(8,128)(2,1)} %param.23) | copy-start | bytes 3538948
  33.5 1.8 %copy-start.8 = (f32[512,192]{0,1:T(8,128)}, f32[512,192]{0,1:T(8,128)S(1)}, u32[]{:S(2)}) copy-start(f32[512,192]{0,1:T(8,128)S(1)} %copy.57) | copy-start | bytes 1179652
  35.3 1.4 copy-start.13
  35.7 1.3 copy-start.14
  59.9 2.3 %copy-start.19 = (bf16[4,768,192]{1,2,0:T(8,128)(2,1)S(1)}, bf16[4,768,192]{1,2,0:T(8,128)(2,1)}, u32[]{:S(2)}) copy-start(bf16[4,768,192]{1,2,0:T(8,128)(2,1)} %param.24) | copy-start | bytes 3538948
  63.8 2.4 %copy-start.9 = (f32[512,192]{0,1:T(8,128)S(1)}, f32[512,192]{0,1:T(8,128)}, u32[]{:S(2)}) copy-start(f32[512,192]{0,1:T(8,128)} %copy-done.8) | copy-start | bytes 1179652
  93.8 5.7 %copy-start.11 = (bf16[192,768]{1,0:T(8,128)(2,1)S(1)}, bf16[192,768]{1,0:T(8,128)(2,1)}, u32[]{:S(2)}) copy-start(bf16[192,768]{1,0:T(8,128)(2,1)} %param.25) | copy-start | bytes 884740
  99.5 1.4 copy-start.3
  102.7 2.9 %copy-start.6 = (bf16[4,128,4,192]{1,0,3,2:T(4,128)(2,1)S(1)}, bf16[4,128,4,192]{1,0,3,2:T(4,128)(2,1)}, u32[]{:S(2)}) copy-start(bf16[4,128,4,192]{1,0,3,2:T(4,128)(2,1)} %copy.67) | copy-start | bytes 2359300
  105.6 3.4 %copy-start.7 = (bf16[2,4,208,128]{3,2,1,0:T(8,128)(2,1)S(1)}, bf16[2,4,208,128]{3,2,1,0:T(8,128)(2,1)}, u32[]{:S(2)}) copy-start(bf16[2,4,208,128]{3,2,1,0:T(8,128)(2,1)} %get-tuple-element.21) | copy-start | bytes 1277956
  109.0 24.0 %copy-start.17 = (s32[32,2]{0,1:T(2,128)S(1)}, s32[32,2]{0,1:T(2,128)}, u32[]{:S(2)}) copy-start(s32[32,2]{0,1:T(2,128)} %param.32) | copy-start | bytes 772
  109.0 24.7 %copy-start.18 = (s32[2,1,256]{2,1,0:T(1,128)S(1)}, s32[2,1,256]{2,1,0:T(1,128)}, u32[]{:S(2)}) copy-start(s32[2,1,256]{2,1,0:T(1,128)} %get-tuple-element.25) | copy-start | bytes 6148
  136.4 7.9 %copy-start.12 = (bf16[128,768]{1,0:T(8,128)(2,1)S(1)}, bf16[128,768]{1,0:T(8,128)(2,1)}, u32[]{:S(2)}) copy-start(bf16[128,768]{1,0:T(8,128)(2,1)} %get-tuple-element.22) | copy-start | bytes 589828
